TPU v7x, 32 devices: a whole 2x2x4 slice. The times are simulated.
32 devices in a mesh: grp: 2 (over y), sp: 16 (over z, x, core).
Axes of the slice: x: 2, y: 2, z: 4, core: 2. Of those that a mesh axis runs over, the one named last changes fastest.
Arguments:
- alpha: float32 [20, 16, 4096], P('grp', None, 'sp'), may hold values from -6 to 6
- ensemble: bfloat16 [20, 3, 16, 4096], P('grp', None, None, 'sp'), may hold values from -6 to 6
- static_std: float32 [3, 16, 4096], P(None, 'grp', 'sp'), may hold values from 0.2 to 1
- control: float32 [3, 16, 4096], P(None, 'grp', 'sp'), may hold values from -6 to 6
- loc_spectrum: float32 [1024], replicated, may hold values from 0.00024414062 to 0.001953125
- obs_cell: int32 [32768], P(('grp', 'sp')), may hold values from 0 to 65535, as said below
- obs_step: int32 [32768], P(('grp', 'sp')), may hold values from 0 to 2
- innovation: float32 [32768], P(('grp', 'sp')), may hold values from -6 to 6
- obs_weight: float32 [32768], P(('grp', 'sp')), may hold values from 0.5 to 4
Outputs:
- grad_alpha: float32 [20, 16, 4096], P('grp', None, 'sp')
- grad_control: float32 [3, 16, 4096], P(None, 'grp', 'sp')
Inputs may be any that keep to these rules, and one draw needn't show every extreme that they name: `obs_cell`: an entry is row * 4096 + column. Entries 1024 * b to 1024 * (b + 1) - 1 lie in the tile of 8 rows from row 8 * (b // 16) and 256 columns from column 256 * (b % 16).
All inputs are finite; a program needn't handle non-finite values.
Results may differ from a plain program's by a relative error of at most 0.0075.
Values may be sent and summed in bfloat16 or wider, within the bound.
A program may use at most 128 MiB of HBM per device.

v0:
```python
import math

import jax
import jax.numpy as jnp
from jax import lax
from jax.sharding import PartitionSpec as P

NX = 4096


courant = 0.4


def extended(block, sides, width):
    for axis, dim in sides:
        count = lax.axis_size(axis)
        forward = [(i, i + 1) for i in range(count - 1)]
        forward.append((count - 1, 0))
        backward = [(target, source) for source, target in forward]
        low = lax.ppermute(
            lax.slice_in_dim(block, block.shape[dim] - width, None, axis=dim), axis, forward
        )
        high = lax.ppermute(lax.slice_in_dim(block, 0, width, axis=dim), axis, backward)
        block = jnp.concatenate([low, block, high], axis=dim)
    return block


def spectral_filter(rows_data, loc_spectrum):
    length_x = rows_data.shape[1]
    kept_waves = loc_spectrum.shape[0]
    freq_block = math.gcd(kept_waves, 256)
    positions = jnp.arange(length_x, dtype=jnp.int32)
    filtered = jnp.zeros(rows_data.shape, jnp.float32)
    for start_wave in range(0, kept_waves, freq_block):
        waves = start_wave + jnp.arange(freq_block, dtype=jnp.int32)
        phases = positions[:, None] * waves[None, :] % length_x
        radians = 2.0 * math.pi / length_x * phases.astype(jnp.float32)
        fourier_basis = jnp.concatenate([jnp.cos(radians), jnp.sin(radians)], axis=1)
        weights = loc_spectrum[start_wave : start_wave + freq_block]
        weights = jnp.concatenate([weights, weights])
        coeffs = jnp.dot(
            rows_data,
            fourier_basis,
            precision=lax.Precision.HIGHEST,
            preferred_element_type=jnp.float32,
        )
        filtered = filtered + jnp.dot(
            coeffs * weights[None, :],
            fourier_basis.T,
            precision=lax.Precision.HIGHEST,
            preferred_element_type=jnp.float32,
        )
    return filtered


def inner(field):
    return field[..., 1:-1, 1:-1]


def diff_x(field):
    return 0.5 * (field[..., 1:-1, 2:] - field[..., 1:-1, :-2])


def diff_y(field):
    return 0.5 * (field[..., 2:, 1:-1] - field[..., :-2, 1:-1])


def clip_rows(stack, margin, first_row, total_rows):
    rows_index = first_row - margin + jnp.arange(stack.shape[1], dtype=jnp.int32)
    valid = jnp.logical_and(rows_index >= 0, rows_index < total_rows).astype(jnp.float32)
    return stack * valid[None, :, None]


def coriolis_rows(first_row, margin, count, total_rows):
    rows_index = first_row - margin + jnp.arange(count, dtype=jnp.int32)
    return (0.1 + 0.2 * (rows_index.astype(jnp.float32) + 0.5) / total_rows)[:, None]


def forward_a(stack, margin, first_row, total_rows):
    height, eastward, northward = (stack[0], stack[1], stack[2])
    new_height = inner(height) - courant * (diff_x(eastward) + diff_y(northward))
    result = jnp.stack([new_height, inner(eastward), inner(northward)])
    return clip_rows(result, margin - 1, first_row, total_rows)


def forward_b(stack, margin, first_row, total_rows):
    height, eastward, northward = (stack[0], stack[1], stack[2])
    rotation = coriolis_rows(first_row, margin - 1, stack.shape[1] - 2, total_rows)
    new_east = inner(eastward) - courant * diff_x(height) + rotation * inner(northward)
    new_north = inner(northward) - courant * diff_y(height) - rotation * inner(eastward)
    result = jnp.stack([inner(height), new_east, new_north])
    return clip_rows(result, margin - 1, first_row, total_rows)


def backward_a(stack, margin, first_row, total_rows):
    back_h, back_u, back_w = (stack[0], stack[1], stack[2])
    adj_height = inner(back_h) + courant * (diff_x(back_u) + diff_y(back_w))
    result = jnp.stack([adj_height, inner(back_u), inner(back_w)])
    return clip_rows(result, margin - 1, first_row, total_rows)


def backward_b(stack, margin, first_row, total_rows):
    adj_height, back_u, back_w = (stack[0], stack[1], stack[2])
    rotation = coriolis_rows(first_row, margin - 1, stack.shape[1] - 2, total_rows)
    adj_east = inner(back_u) - rotation * inner(back_w) + courant * diff_x(adj_height)
    adj_north = inner(back_w) + rotation * inner(back_u) + courant * diff_y(adj_height)
    result = jnp.stack([inner(adj_height), adj_east, adj_north])
    return clip_rows(result, margin - 1, first_row, total_rows)


def deep_rim(stack):
    return extended(stack, (("grp", 1), ("sp", 2)), 4)


def per_device(
    alpha, ensemble, static_std, control, loc_spectrum, obs_cell, obs_step, innovation, obs_weight
):
    members_local = alpha.shape[0]
    groups = lax.axis_size("grp")
    spread = 1.0 / math.sqrt(members_local * groups - 1)
    tile_rows, tile_cols = (control.shape[1], control.shape[2])
    total_rows = tile_rows * groups
    first_row = lax.axis_index("grp") * tile_rows
    first_col = lax.axis_index("sp") * tile_cols

    def localize_items(items):
        dims = items.shape
        flat = items.reshape(dims[0] * dims[1], dims[2])
        return spectral_filter(flat, loc_spectrum).reshape(dims)

    def to_rows(columns):
        return localize_items(
            lax.all_to_all(columns, "sp", split_axis=1, concat_axis=2, tiled=True)
        )

    localized = lax.all_to_all(
        to_rows(alpha).astype(jnp.bfloat16), "sp", split_axis=2, concat_axis=1, tiled=True
    )
    partial_value = jnp.einsum(
        "mvyx,myx->vyx", ensemble, localized, preferred_element_type=jnp.float32
    )
    summed = lax.psum_scatter(partial_value, "grp", scatter_dimension=1, tiled=True)
    increment = static_std * control + spread * summed
    padded = clip_rows(deep_rim(increment), 4, first_row, total_rows)
    middle = forward_b(forward_a(padded, 4, first_row, total_rows), 3, first_row, total_rows)
    first_state = middle[:, 2:-2, 2:-2]
    second_state = forward_b(forward_a(middle, 2, first_row, total_rows), 1, first_row, total_rows)
    states = (increment, first_state, second_state)
    local_index = (obs_cell // NX - first_row) * tile_cols + (obs_cell % NX - first_col)
    observed = jnp.zeros(innovation.shape, jnp.float32)
    for moment in range(3):
        values = states[moment][0].reshape(-1)[local_index]
        observed = jnp.where(obs_step == moment, values, observed)
    misfit = obs_weight * (observed - innovation)
    forcings = []
    for moment in range(3):
        spread_obs = jnp.where(obs_step == moment, misfit, jnp.zeros_like(misfit))
        height_force = (
            jnp.zeros((tile_rows * tile_cols,), jnp.float32).at[local_index].add(spread_obs)
        )
        forcings.append(height_force.reshape(tile_rows, tile_cols))
    zero_field = jnp.zeros((tile_rows, tile_cols), jnp.float32)
    last_adjoint = jnp.stack([forcings[2], zero_field, zero_field])
    padded = clip_rows(
        deep_rim(jnp.concatenate([last_adjoint, forcings[1][None]], axis=0)),
        4,
        first_row,
        total_rows,
    )
    middle = backward_b(backward_a(padded[:3], 4, first_row, total_rows), 3, first_row, total_rows)
    middle = middle.at[0].add(padded[3, 2:-2, 2:-2])
    adjoint = backward_b(backward_a(middle, 2, first_row, total_rows), 1, first_row, total_rows)
    adjoint = adjoint.at[0].add(forcings[0])
    grad_control = control + static_std * adjoint
    half = adjoint.astype(jnp.bfloat16)
    weighted = jnp.einsum(
        "mvyx,vyx->myx",
        ensemble,
        lax.all_gather(half, "grp", axis=1, tiled=True),
        preferred_element_type=jnp.float32,
    )
    filtered = lax.all_to_all(to_rows(weighted), "sp", split_axis=2, concat_axis=1, tiled=True)
    grad_alpha = alpha + spread * filtered
    return (grad_alpha, grad_control)


def solution(mesh):
    placed = (
        P("grp", None, "sp"),
        P("grp", None, None, "sp"),
        P(None, "grp", "sp"),
        P(None, "grp", "sp"),
        P(),
        P(("grp", "sp")),
        P(("grp", "sp")),
        P(("grp", "sp")),
        P(("grp", "sp")),
    )
    return jax.shard_map(
        per_device,
        mesh=mesh,
        in_specs=placed,
        out_specs=(P("grp", None, "sp"), P(None, "grp", "sp")),
        check_vma=False,
    )
```

profile of v0, /device:TPU:0, one launch (start us, length us, event | category | flops | bytes accessed | tf_op | source)
XLA Modules:
  0.0 365.7 jit_solution(6767588958854362796)
XLA Ops:
  7.2 1.7 copy.22
  8.9 7.4 %all-to-all-start = ((f32[10,16,256]{2,0,1:T(8,128)}), f32[10,16,256]{2,0,1:T(8,128)S(1)}, u32[]{:S(2)}, u32[]{:S(2)}) async-start(f32[10,16,256]{2,0,1:T(8,128)} %copy.22), calls=%async_computation | async-start | bytes 524288 | tf_op jit(solution)/shard_map/all_to_all | solution.py:133
  16.3 17.6 %fusion.37 = (f32[4096,256]{1,0:T(8,128)}, f32[4096,256]{1,0:T(8,128)}) fusion(), kind=kLoop, calls=%fused_computation.65 | loop fusion | flops 14680064 | bytes 8388608 | tf_op jit(solution)/shard_map/sin | solution.py:38
  34.0 17.9 %fusion.44 = (f32[4096,256]{1,0:T(8,128)}, f32[4096,256]{1,0:T(8,128)}) fusion(s32[256]{0:T(256)S(1)} %iota_add_fusion.2), kind=kLoop, calls=%fused_computation.72 | loop fusion | flops 14680064 | bytes 8389632 | tf_op jit(solution)/shard_map/cos | solution.py:38
  51.8 17.9 %fusion.42 = (f32[4096,256]{1,0:T(8,128)}, f32[4096,256]{1,0:T(8,128)}) fusion(s32[256]{0:T(256)S(1)} %iota_add_fusion.1), kind=kLoop, calls=%fused_computation.70 | loop fusion | flops 14680064 | bytes 8389632 | tf_op jit(solution)/shard_map/cos | solution.py:38
  69.7 17.9 %fusion.40 = (f32[4096,256]{1,0:T(8,128)}, f32[4096,256]{1,0:T(8,128)}) fusion(s32[256]{0:T(256)S(1)} %iota_add_fusion), kind=kLoop, calls=%fused_computation.68 | loop fusion | flops 14680064 | bytes 8389632 | tf_op jit(solution)/shard_map/cos | solution.py:38
  87.8 0.2 copy.46
  88.0 7.5 %fusion.45 = f32[512,10]{0,1:T(8,128)S(1)} fusion(f32[10,4096]{1,0:T(8,128)S(1)} %bitcast.175, f32[4096,256]{1,0:T(8,128)} %get-tuple-element.106, f32[4096,256]{1,0:T(8,128)} %get-tuple-element.107, f32[512]{0:T(512)S(1)} %get-tuple-element.102), kind=kOutput, calls=%fused_computation.73 | convolution fusion | flops 253760512 | bytes 8574976 | tf_op jit(solution)/shard_map/dot_general | solution.py:41
  95.5 7.0 %fusion.35 = f32[10,4096]{1,0:T(8,128)S(1)} fusion(f32[512,10]{0,1:T(8,128)S(1)} %fusion.45, f32[4096,256]{1,0:T(8,128)S(1)} %copy-done, f32[4096,256]{1,0:T(8,128)S(1)} %copy-done.2), kind=kOutput, calls=%fused_computation.63 | convolution fusion | flops 253755392 | bytes 8572928 | tf_op jit(solution)/shard_map/dot_general | solution.py:47
  102.5 4.5 %fusion.47 = f32[512,10]{0,1:T(8,128)S(1)} fusion(f32[10,4096]{1,0:T(8,128)S(1)} %bitcast.176, f32[4096,256]{1,0:T(8,128)S(1)} %copy-done.14, f32[4096,256]{1,0:T(8,128)S(1)} %copy-done.12, f32[512]{0:T(512)S(1)} %get-tuple-element.103), kind=kOutput, calls=%fused_computation.75 | convolution fusion | flops 253760512 | bytes 8574976 | tf_op jit(solution)/shard_map/dot_general | solution.py:41
  107.0 7.2 %convolution_add_fusion.5 = f32[10,4096]{1,0:T(8,128)S(1)} fusion(f32[10,4096]{1,0:T(8,128)S(1)} %fusion.35, f32[512,10]{0,1:T(8,128)S(1)} %fusion.47, f32[4096,256]{1,0:T(8,128)S(1)} %copy-done.14, f32[4096,256]{1,0:T(8,128)S(1)} %copy-done.12), kind=kOutput, calls=%fused_computation.28 | convolution fusion | flops 253796352 | bytes 8736768 | tf_op jit(solution)/shard_map/dot_general | solution.py:47
  114.2 4.5 %fusion.49 = f32[512,10]{0,1:T(8,128)S(1)} fusion(f32[10,4096]{1,0:T(8,128)S(1)} %bitcast.177, f32[4096,256]{1,0:T(8,128)S(1)} %copy-done.10, f32[4096,256]{1,0:T(8,128)S(1)} %copy-done.8, f32[512]{0:T(512)S(1)} %get-tuple-element.104), kind=kOutput, calls=%fused_computation.77 | convolution fusion | flops 253760512 | bytes 8574976 | tf_op jit(solution)/shard_map/dot_general | solution.py:41
  118.7 7.4 %convolution_add_fusion.4 = f32[10,4096]{1,0:T(8,128)S(1)} fusion(f32[10,4096]{1,0:T(8,128)S(1)} %convolution_add_fusion.5, f32[512,10]{0,1:T(8,128)S(1)} %fusion.49, f32[4096,256]{1,0:T(8,128)S(1)} %copy-done.10, f32[4096,256]{1,0:T(8,128)S(1)} %copy-done.8), kind=kOutput, calls=%fused_computation.27 | convolution fusion | flops 253796352 | bytes 8736768 | tf_op jit(solution)/shard_map/dot_general | solution.py:47
  126.2 4.5 %fusion.51 = f32[512,10]{0,1:T(8,128)S(1)} fusion(f32[10,4096]{1,0:T(8,128)S(1)} %bitcast.178, f32[4096,256]{1,0:T(8,128)S(1)} %copy-done.6, f32[4096,256]{1,0:T(8,128)S(1)} %copy-done.4, f32[512]{0:T(512)S(1)} %get-tuple-element.105), kind=kOutput, calls=%fused_computation.79 | convolution fusion | flops 253760512 | bytes 8574976 | tf_op jit(solution)/shard_map/dot_general | solution.py:41
  130.7 7.2 %fusion.2 = bf16[10,1,4096]{2,0,1:T(8,128)(2,1)S(1)} fusion(f32[10,4096]{1,0:T(8,128)S(1)} %convolution_add_fusion.4, f32[512,10]{0,1:T(8,128)S(1)} %fusion.51, f32[4096,256]{1,0:T(8,128)S(1)} %copy-done.6, f32[4096,256]{1,0:T(8,128)S(1)} %copy-done.4), kind=kOutput, calls=%fused_computation.30 | convolution fusion | flops 253837312 | bytes 8654848 | tf_op jit(solution)/shard_map/dot_general | solution.py:47
  137.8 2.8 copy.24
  140.6 0.5 broadcast.393
  141.2 22.5 %reduce.10 = bf16[4096,10]{1,0:T(8,128)(2,1)S(1)} reduce(bf16[4096,1,10]{2,1,0:T(2,128)(2,1)S(1)} %bitcast.160, bf16[]{:T(256)} %broadcast.393), dimensions={1}, to_apply=%bitcast.136.reduce_sub_computation | reduce | bytes 163842
  163.6 2.5 reshape.233
  166.1 6.0 %all-to-all-start.1 = ((bf16[16,2,1280]{2,1,0:T(2,128)(2,1)}), bf16[16,2,1280]{2,1,0:T(2,128)(2,1)S(1)}, u32[]{:S(2)}, u32[]{:S(2)}) async-start(bf16[16,2,1280]{2,1,0:T(2,128)(2,1)} %reshape.233), calls=%async_computation.1 | async-start | bytes 163840 | tf_op jit(solution)/shard_map/all_to_all | solution.py:136
  172.2 7.0 %all-to-all-done.1 = bf16[16,2,1280]{2,1,0:T(2,128)(2,1)S(1)} async-done(((bf16[16,2,1280]{2,1,0:T(2,128)(2,1)}), bf16[16,2,1280]{2,1,0:T(2,128)(2,1)S(1)}, u32[]{:S(2)}, u32[]{:S(2)}) %all-to-all-start.1) | async-done | bytes 81952 | tf_op jit(solution)/shard_map/all_to_all | solution.py:136
  179.2 2.2 reshape.234
  181.4 2.1 copy.25
  183.6 0.7 multiply_reduce_fusion.1
  184.4 7.6 %reduce-scatter.2.cloned.1.call-done = f32[3,8,256]{2,1,0:T(8,128)} async-done(((f32[3,16,256]{2,1,0:T(8,128)}), f32[3,8,256]{2,1,0:T(8,128)}) %reduce-scatter.2.cloned.1.call-update) | async-done | bytes 24592 | tf_op jit(solution)/shard_map/reduce_scatter | solution.py:142
  192.0 0.7 multiply_add_fusion.1
  192.7 0.2 collective-permute-start
  193.0 1.8 collective-permute-start.1
  194.8 1.7 collective-permute-done
  196.5 0.2 collective-permute-done.1
  196.8 4.4 %collective-permute-start.3 = (f32[3,16,4]{2,1,0:T(8,128)S(1)}, f32[3,16,4]{2,1,0:T(8,128)S(1)}, u32[]{:S(2)}, u32[]{:S(2)}) collective-permute-start(f32[3,16,4]{2,1,0:T(8,128)S(1)} %get-tuple-element.67), channel_id=1, source_target_pairs={{1,0},{2,1},{3,2},{4,3},{5,4},{6,5},{7,6},{8,7},{9,8},{10,9},{11,1... | collective-permute-start | bytes 2312 | tf_op jit(solution)/shard_map/ppermute | solution.py:23
  201.2 6.1 %gather_fusion.2 = f32[1024]{0:T(1024)S(1)} fusion(f32[2048]{0:T(1024)S(1)} %bitcast.158, s32[1024]{0:T(1024)S(1)} %get-tuple-element.30), kind=kCustom, calls=%fused_computation.2 | custom fusion | bytes 12288 | tf_op jit(solution)/shard_map/gather | solution.py:152
  208.4 6.2 %gather_fusion = f32[1024]{0:T(1024)S(1)} fusion(f32[2048]{0:T(1024)S(1)} %bitcast.159, s32[1024]{0:T(1024)S(1)} %get-tuple-element.30), kind=kCustom, calls=%fused_computation | custom fusion | bytes 12288 | tf_op jit(solution)/shard_map/gather | solution.py:152
  214.6 6.2 %gather_fusion.1 = f32[1024]{0:T(1024)S(1)} fusion(f32[2048]{0:T(1024)S(1)} %bitcast.157, s32[1024]{0:T(1024)S(1)} %get-tuple-element.30), kind=kCustom, calls=%fused_computation.1 | custom fusion | bytes 12288 | tf_op jit(solution)/shard_map/gather | solution.py:152
  220.8 6.0 %scatter_custom_fusion = f32[2048]{0:T(1024)S(1)} fusion(s32[1024]{0:T(1024)S(1)} %get-tuple-element.31, f32[1024]{0:T(1024)S(1)} %get-tuple-element.90, f32[]{:T(128)} %constant.175.clone.1), kind=kCustom, calls=%fused_computation.226 | custom fusion | flops 1024 | bytes 8196 | tf_op jit(solution)/shard_map/scatter-add | solution.py:159
  226.8 6.0 %scatter_custom_fusion.1 = f32[2048]{0:T(1024)S(1)} fusion(s32[1024]{0:T(1024)S(1)} %get-tuple-element.31, f32[1024]{0:T(1024)S(1)} %get-tuple-element.91, f32[]{:T(128)} %constant.175.clone.1), kind=kCustom, calls=%fused_computation.224 | custom fusion | flops 1024 | bytes 8196 | tf_op jit(solution)/shard_map/scatter-add | solution.py:159
  232.8 1.9 collective-permute-start.4
  234.7 0.2 collective-permute-start.5
  234.9 1.7 collective-permute-done.4
  236.6 1.8 collective-permute-done.5
  238.5 4.4 %collective-permute-start.7 = (f32[4,16,4]{2,1,0:T(8,128)S(1)}, f32[4,16,4]{2,1,0:T(8,128)S(1)}, u32[]{:S(2)}, u32[]{:S(2)}) collective-permute-start(f32[4,16,4]{2,1,0:T(8,128)S(1)} %get-tuple-element.65), channel_id=1, source_target_pairs={{1,0},{2,1},{3,2},{4,3},{5,4},{6,5},{7,6},{8,7},{9,8},{10,9},{11,1... | collective-permute-start | bytes 3080 | tf_op jit(solution)/shard_map/ppermute | solution.py:23
  242.9 6.0 %scatter_custom_fusion.2 = f32[2048]{0:T(1024)S(1)} fusion(s32[1024]{0:T(1024)S(1)} %get-tuple-element.31, f32[1024]{0:T(1024)S(1)} %get-tuple-element.26, f32[]{:T(128)} %constant.175.clone.1), kind=kCustom, calls=%fused_computation.222 | custom fusion | flops 1024 | bytes 8196 | tf_op jit(solution)/shard_map/scatter-add | solution.py:159
  250.0 0.6 multiply_add_fusion
  250.6 4.4 %all_gather.3 = bf16[3,16,256]{2,1,0:T(8,128)(2,1)S(1)} all-gather(bf16[3,8,256]{2,1,0:T(8,128)(2,1)S(1)} %get-tuple-element.71), channel_id=1, replica_groups=mesh['grp'=2,'sp'=16] {'grp'}, dimensions={1}, use_global_device_ids=true | all-gather | bytes 36864 | tf_op jit(solution)/shard_map/all_gather | solution.py:179
  255.1 12.6 %all_to_all.19 = f32[10,16,256]{2,0,1:T(8,128)S(1)} all-to-all(f32[10,16,256]{2,0,1:T(8,128)S(1)} %bitcast.170), channel_id=1, replica_groups=mesh['grp'=2,'sp'=16] {'sp'}, dimensions={1} | all-to-all | bytes 327680 | tf_op jit(solution)/shard_map/all_to_all | solution.py:133
  267.9 0.2 copy.51
  268.1 4.9 %fusion.52 = f32[10,512]{1,0:T(8,128)S(1)} fusion(f32[10,4096]{1,0:T(8,128)S(1)} %bitcast.164, f32[4096,256]{1,0:T(8,128)} %get-tuple-element.97, f32[4096,256]{1,0:T(8,128)S(1)} %copy-done.5, f32[512]{0:T(512)S(1)} %get-tuple-element.105), kind=kOutput, calls=%fused_computation.80 | convolution fusion | flops 253760512 | bytes 8574976 | tf_op jit(solution)/shard_map/dot_general | solution.py:41
  273.0 4.1 %fusion.50 = f32[10,512]{1,0:T(8,128)S(1)} fusion(f32[10,4096]{1,0:T(8,128)S(1)} %bitcast.165, f32[4096,256]{1,0:T(8,128)S(1)} %copy-done.11, f32[4096,256]{1,0:T(8,128)S(1)} %copy-done.9, f32[512]{0:T(512)S(1)} %get-tuple-element.104), kind=kOutput, calls=%fused_computation.78 | convolution fusion | flops 253760512 | bytes 8574976 | tf_op jit(solution)/shard_map/dot_general | solution.py:41
  277.1 4.1 %fusion.48 = f32[10,512]{1,0:T(8,128)S(1)} fusion(f32[10,4096]{1,0:T(8,128)S(1)} %bitcast.166, f32[4096,256]{1,0:T(8,128)S(1)} %copy-done.15, f32[4096,256]{1,0:T(8,128)S(1)} %copy-done.13, f32[512]{0:T(512)S(1)} %get-tuple-element.103), kind=kOutput, calls=%fused_computation.76 | convolution fusion | flops 253760512 | bytes 8574976 | tf_op jit(solution)/shard_map/dot_general | solution.py:41
  281.2 4.3 %fusion.46 = f32[10,512]{1,0:T(8,128)S(1)} fusion(f32[10,4096]{1,0:T(8,128)S(1)} %bitcast.167, f32[4096,256]{1,0:T(8,128)S(1)} %copy-done.1, f32[4096,256]{1,0:T(8,128)S(1)} %copy-done.3, f32[512]{0:T(512)S(1)} %get-tuple-element.102), kind=kOutput, calls=%fused_computation.74 | convolution fusion | flops 253760512 | bytes 8574976 | tf_op jit(solution)/shard_map/dot_general | solution.py:41
  285.4 7.0 %fusion.33 = f32[10,4096]{1,0:T(8,128)S(1)} fusion(f32[10,512]{1,0:T(8,128)S(1)} %fusion.46, f32[4096,256]{1,0:T(8,128)S(1)} %copy-done.1, f32[4096,256]{1,0:T(8,128)S(1)} %copy-done.3), kind=kOutput, calls=%fused_computation.61 | convolution fusion | flops 253755392 | bytes 8572928 | tf_op jit(solution)/shard_map/dot_general | solution.py:47
  292.4 7.2 %convolution_add_fusion.2 = f32[10,4096]{1,0:T(8,128)S(1)} fusion(f32[10,4096]{1,0:T(8,128)S(1)} %fusion.33, f32[10,512]{1,0:T(8,128)S(1)} %fusion.48, f32[4096,256]{1,0:T(8,128)S(1)} %copy-done.15, f32[4096,256]{1,0:T(8,128)S(1)} %copy-done.13), kind=kOutput, calls=%fused_computation.25 | convolution fusion | flops 253796352 | bytes 8736768 | tf_op jit(solution)/shard_map/dot_general | solution.py:47
  299.6 7.0 %convolution_add_fusion.1 = f32[10,4096]{1,0:T(8,128)S(1)} fusion(f32[10,4096]{1,0:T(8,128)S(1)} %convolution_add_fusion.2, f32[10,512]{1,0:T(8,128)S(1)} %fusion.50, f32[4096,256]{1,0:T(8,128)S(1)} %copy-done.11, f32[4096,256]{1,0:T(8,128)S(1)} %copy-done.9), kind=kOutput, calls=%fused_computation.24 | convolution fusion | flops 253796352 | bytes 8736768 | tf_op jit(solution)/shard_map/dot_general | solution.py:47
  306.7 7.0 %fusion = f32[10,1,4096]{2,0,1:T(8,128)S(1)} fusion(f32[10,4096]{1,0:T(8,128)S(1)} %convolution_add_fusion.1, f32[10,512]{1,0:T(8,128)S(1)} %fusion.52, f32[4096,256]{1,0:T(8,128)S(1)} %copy-done.7, f32[4096,256]{1,0:T(8,128)S(1)} %copy-done.5), kind=kOutput, calls=%fused_computation.23 | convolution fusion | flops 253796352 | bytes 8736768 | tf_op jit(solution)/shard_map/dot_general | solution.py:47
  313.7 2.5 copy.27
  316.2 0.5 broadcast.394
  316.7 19.6 %reduce.11 = f32[4096,10]{1,0:T(8,128)} reduce(f32[4096,1,10]{2,1,0:T(1,128)S(1)} %bitcast.161, f32[]{:T(128)} %broadcast.394), dimensions={1}, to_apply=%bitcast.138.reduce_sub_computation | reduce | bytes 327684
  336.3 3.4 reshape.235
  339.8 11.1 %all_to_all.40 = f32[16,1,2560]{2,1,0:T(1,128)S(1)} all-to-all(f32[16,1,2560]{2,1,0:T(1,128)S(1)} %reshape.235), channel_id=1, replica_groups=mesh['grp'=2,'sp'=16] {'sp'}, dimensions={0} | all-to-all | bytes 327680 | tf_op jit(solution)/shard_map/all_to_all | solution.py:182
  350.9 1.0 reduce.12
  351.9 3.3 reshape.236
  355.2 2.0 copy.28
  357.2 0.5 multiply_reduce_fusion.2
  357.7 0.7 slice_add_fusion
  (128 shorter events, 3.0 us)
Async XLA Ops:
  8.9 78.7 %all-to-all-start = ((f32[10,16,256]{2,0,1:T(8,128)}), f32[10,16,256]{2,0,1:T(8,128)S(1)}, u32[]{:S(2)}, u32[]{:S(2)}) async-start(f32[10,16,256]{2,0,1:T(8,128)} %copy.22), calls=%async_computation | async-start | bytes 524288 | tf_op jit(solution)/shard_map/all_to_all | solution.py:133
  16.3 17.7 %copy-start.23 = (f32[1024]{0:T(1024)S(1)}, f32[1024]{0:T(1024)}, u32[]{:S(2)}) copy-start(f32[1024]{0:T(1024)} %param.17) | copy-start | bytes 12292
  69.7 17.9 %copy-start.24 = (s32[1024]{0:T(1024)S(1)}, s32[1024]{0:T(1024)}, u32[]{:S(2)}) copy-start(s32[1024]{0:T(1024)} %param.18) | copy-start | bytes 12292
  87.9 7.5 %copy-start = (f32[4096,256]{1,0:T(8,128)S(1)}, f32[4096,256]{1,0:T(8,128)}, u32[]{:S(2)}) copy-start(f32[4096,256]{1,0:T(8,128)} %get-tuple-element.106) | copy-start | bytes 12582916
  87.9 7.5 %copy-start.2 = (f32[4096,256]{1,0:T(8,128)S(1)}, f32[4096,256]{1,0:T(8,128)}, u32[]{:S(2)}) copy-start(f32[4096,256]{1,0:T(8,128)} %get-tuple-element.107) | copy-start | bytes 12582916
  95.5 7.0 %copy-start.12 = (f32[4096,256]{1,0:T(8,128)S(1)}, f32[4096,256]{1,0:T(8,128)}, u32[]{:S(2)}) copy-start(f32[4096,256]{1,0:T(8,128)} %get-tuple-element.100) | copy-start | bytes 12582916
  95.5 7.0 %copy-start.14 = (f32[4096,256]{1,0:T(8,128)S(1)}, f32[4096,256]{1,0:T(8,128)}, u32[]{:S(2)}) copy-start(f32[4096,256]{1,0:T(8,128)} %get-tuple-element.101) | copy-start | bytes 12582916
  107.0 7.2 %copy-start.8 = (f32[4096,256]{1,0:T(8,128)S(1)}, f32[4096,256]{1,0:T(8,128)}, u32[]{:S(2)}) copy-start(f32[4096,256]{1,0:T(8,128)} %get-tuple-element.98) | copy-start | bytes 12582916
  107.0 7.2 %copy-start.10 = (f32[4096,256]{1,0:T(8,128)S(1)}, f32[4096,256]{1,0:T(8,128)}, u32[]{:S(2)}) copy-start(f32[4096,256]{1,0:T(8,128)} %get-tuple-element.99) | copy-start | bytes 12582916
  118.7 7.4 %copy-start.4 = (f32[4096,256]{1,0:T(8,128)S(1)}, f32[4096,256]{1,0:T(8,128)}, u32[]{:S(2)}) copy-start(f32[4096,256]{1,0:T(8,128)} %get-tuple-element.96) | copy-start | bytes 12582916
  118.7 7.4 %copy-start.6 = (f32[4096,256]{1,0:T(8,128)S(1)}, f32[4096,256]{1,0:T(8,128)}, u32[]{:S(2)}) copy-start(f32[4096,256]{1,0:T(8,128)} %get-tuple-element.97) | copy-start | bytes 12582916
  141.2 42.5 %copy-start.16 = (bf16[10,3,16,256]{3,2,1,0:T(8,128)(2,1)S(1)}, bf16[10,3,16,256]{3,2,1,0:T(8,128)(2,1)}, u32[]{:S(2)}) copy-start(bf16[10,3,16,256]{3,2,1,0:T(8,128)(2,1)} %param.14) | copy-start | bytes 737284
  141.2 50.8 %copy-start.18 = (f32[3,8,256]{2,1,0:T(8,128)S(1)}, f32[3,8,256]{2,1,0:T(8,128)}, u32[]{:S(2)}) copy-start(f32[3,8,256]{2,1,0:T(8,128)} %param.16) | copy-start | bytes 73732
  141.2 50.8 %copy-start.19 = (f32[3,8,256]{2,1,0:T(8,128)S(1)}, f32[3,8,256]{2,1,0:T(8,128)}, u32[]{:S(2)}) copy-start(f32[3,8,256]{2,1,0:T(8,128)} %param.15) | copy-start | bytes 73732
  166.1 13.1 %all-to-all-start.1 = ((bf16[16,2,1280]{2,1,0:T(2,128)(2,1)}), bf16[16,2,1280]{2,1,0:T(2,128)(2,1)S(1)}, u32[]{:S(2)}, u32[]{:S(2)}) async-start(bf16[16,2,1280]{2,1,0:T(2,128)(2,1)} %reshape.233), calls=%async_computation.1 | async-start | bytes 163840 | tf_op jit(solution)/shard_map/all_to_all | solution.py:136
  172.1 19.9 %reduce-scatter.2.cloned.1.call-start = ((), (), s32[]{:S(2)}) async-start(), calls=%async_computation.5 | async-start | bytes 73728 | tf_op jit(solution)/shard_map/reduce_scatter | solution.py:142
  192.7 3.8 %collective-permute-start = (f32[3,4,256]{2,1,0:T(4,128)S(1)}, f32[3,4,256]{2,1,0:T(4,128)S(1)}, u32[]{:S(2)}, u32[]{:S(2)}) collective-permute-start(f32[3,4,256]{2,1,0:T(4,128)S(1)} %get-tuple-element.88), channel_id=1, source_target_pairs={{0,16},{16,0},{1,17},{17,1},{2,18},{18,2},{3,19},{19,3},{4,20},{20... | collective-permute-start | bytes 36872 | tf_op jit(solution)/shard_map/ppermute | solution.py:20
  193.0 3.7 %collective-permute-start.1 = (f32[3,4,256]{2,1,0:T(4,128)S(1)}, f32[3,4,256]{2,1,0:T(4,128)S(1)}, u32[]{:S(2)}, u32[]{:S(2)}) collective-permute-start(f32[3,4,256]{2,1,0:T(4,128)S(1)} %get-tuple-element.89), channel_id=1, source_target_pairs={{16,0},{0,16},{17,1},{1,17},{18,2},{2,18},{19,3},{3,19},{20,4},{4,... | collective-permute-start | bytes 36872 | tf_op jit(solution)/shard_map/ppermute | solution.py:23
  196.7 10.6 %collective-permute-start.2 = (f32[3,16,4]{2,1,0:T(8,128)S(1)}, f32[3,16,4]{2,1,0:T(8,128)S(1)}, u32[]{:S(2)}, u32[]{:S(2)}) collective-permute-start(f32[3,16,4]{2,1,0:T(8,128)S(1)} %get-tuple-element.66), channel_id=1, source_target_pairs={{0,1},{1,2},{2,3},{3,4},{4,5},{5,6},{6,7},{7,8},{8,9},{9,10},{10,1... | collective-permute-start | bytes 2312 | tf_op jit(solution)/shard_map/ppermute | solution.py:20
  196.8 10.6 %collective-permute-start.3 = (f32[3,16,4]{2,1,0:T(8,128)S(1)}, f32[3,16,4]{2,1,0:T(8,128)S(1)}, u32[]{:S(2)}, u32[]{:S(2)}) collective-permute-start(f32[3,16,4]{2,1,0:T(8,128)S(1)} %get-tuple-element.67), channel_id=1, source_target_pairs={{1,0},{2,1},{3,2},{4,3},{5,4},{6,5},{7,6},{8,7},{9,8},{10,9},{11,1... | collective-permute-start | bytes 2312 | tf_op jit(solution)/shard_map/ppermute | solution.py:23
  208.4 12.4 %copy-start.20 = (f32[1024]{0:T(1024)S(1)}, f32[1024]{0:T(1024)}, u32[]{:S(2)}) copy-start(f32[1024]{0:T(1024)} %param.21) | copy-start | bytes 12292
  208.4 12.4 %copy-start.21 = (f32[1024]{0:T(1024)S(1)}, f32[1024]{0:T(1024)}, u32[]{:S(2)}) copy-start(f32[1024]{0:T(1024)} %param.20) | copy-start | bytes 12292
  208.4 12.4 %copy-start.22 = (s32[1024]{0:T(1024)S(1)}, s32[1024]{0:T(1024)}, u32[]{:S(2)}) copy-start(s32[1024]{0:T(1024)} %param.19) | copy-start | bytes 12292
  232.8 3.8 %collective-permute-start.4 = (f32[4,4,256]{2,1,0:T(4,128)S(1)}, f32[4,4,256]{2,1,0:T(4,128)S(1)}, u32[]{:S(2)}, u32[]{:S(2)}) collective-permute-start(f32[4,4,256]{2,1,0:T(4,128)S(1)} %get-tuple-element.68), channel_id=1, source_target_pairs={{0,16},{16,0},{1,17},{17,1},{2,18},{18,2},{3,19},{19,3},{4,20},{20... | collective-permute-start | bytes 49160 | tf_op jit(solution)/shard_map/ppermute | solution.py:20
  234.7 3.7 %collective-permute-start.5 = (f32[4,4,256]{2,1,0:T(4,128)S(1)}, f32[4,4,256]{2,1,0:T(4,128)S(1)}, u32[]{:S(2)}, u32[]{:S(2)}) collective-permute-start(f32[4,4,256]{2,1,0:T(4,128)S(1)} %get-tuple-element.69), channel_id=1, source_target_pairs={{16,0},{0,16},{17,1},{1,17},{18,2},{2,18},{19,3},{3,19},{20,4},{4,... | collective-permute-start | bytes 49160 | tf_op jit(solution)/shard_map/ppermute | solution.py:23
  238.5 10.4 %collective-permute-start.6 = (f32[4,16,4]{2,1,0:T(8,128)S(1)}, f32[4,16,4]{2,1,0:T(8,128)S(1)}, u32[]{:S(2)}, u32[]{:S(2)}) collective-permute-start(f32[4,16,4]{2,1,0:T(8,128)S(1)} %get-tuple-element.64), channel_id=1, source_target_pairs={{0,1},{1,2},{2,3},{3,4},{4,5},{5,6},{6,7},{7,8},{8,9},{9,10},{10,1... | collective-permute-start | bytes 3080 | tf_op jit(solution)/shard_map/ppermute | solution.py:20
  238.5 10.4 %collective-permute-start.7 = (f32[4,16,4]{2,1,0:T(8,128)S(1)}, f32[4,16,4]{2,1,0:T(8,128)S(1)}, u32[]{:S(2)}, u32[]{:S(2)}) collective-permute-start(f32[4,16,4]{2,1,0:T(8,128)S(1)} %get-tuple-element.65), channel_id=1, source_target_pairs={{1,0},{2,1},{3,2},{4,3},{5,4},{6,5},{7,6},{8,7},{9,8},{10,9},{11,1... | collective-permute-start | bytes 3080 | tf_op jit(solution)/shard_map/ppermute | solution.py:23
  248.9 19.1 %copy-start.5 = (f32[4096,256]{1,0:T(8,128)S(1)}, f32[4096,256]{1,0:T(8,128)}, u32[]{:S(2)}) copy-start(f32[4096,256]{1,0:T(8,128)} %get-tuple-element.96) | copy-start | bytes 12582916
  268.0 4.9 %copy-start.9 = (f32[4096,256]{1,0:T(8,128)S(1)}, f32[4096,256]{1,0:T(8,128)}, u32[]{:S(2)}) copy-start(f32[4096,256]{1,0:T(8,128)} %get-tuple-element.98) | copy-start | bytes 12582916
  268.0 4.9 %copy-start.11 = (f32[4096,256]{1,0:T(8,128)S(1)}, f32[4096,256]{1,0:T(8,128)}, u32[]{:S(2)}) copy-start(f32[4096,256]{1,0:T(8,128)} %get-tuple-element.99) | copy-start | bytes 12582916
  273.0 4.1 %copy-start.13 = (f32[4096,256]{1,0:T(8,128)S(1)}, f32[4096,256]{1,0:T(8,128)}, u32[]{:S(2)}) copy-start(f32[4096,256]{1,0:T(8,128)} %get-tuple-element.100) | copy-start | bytes 12582916
  273.0 4.1 %copy-start.15 = (f32[4096,256]{1,0:T(8,128)S(1)}, f32[4096,256]{1,0:T(8,128)}, u32[]{:S(2)}) copy-start(f32[4096,256]{1,0:T(8,128)} %get-tuple-element.101) | copy-start | bytes 12582916
  277.1 4.1 %copy-start.1 = (f32[4096,256]{1,0:T(8,128)S(1)}, f32[4096,256]{1,0:T(8,128)}, u32[]{:S(2)}) copy-start(f32[4096,256]{1,0:T(8,128)} %get-tuple-element.106) | copy-start | bytes 12582916
  277.1 4.1 %copy-start.3 = (f32[4096,256]{1,0:T(8,128)S(1)}, f32[4096,256]{1,0:T(8,128)}, u32[]{:S(2)}) copy-start(f32[4096,256]{1,0:T(8,128)} %get-tuple-element.107) | copy-start | bytes 12582916
  299.6 7.0 %copy-start.7 = (f32[4096,256]{1,0:T(8,128)S(1)}, f32[4096,256]{1,0:T(8,128)}, u32[]{:S(2)}) copy-start(f32[4096,256]{1,0:T(8,128)} %get-tuple-element.97) | copy-start | bytes 12582916
  336.3 21.4 %copy-start.17 = (f32[10,16,256]{2,1,0:T(8,128)S(1)}, f32[10,16,256]{2,1,0:T(8,128)}, u32[]{:S(2)}) copy-start(f32[10,16,256]{2,1,0:T(8,128)} %param.13) | copy-start | bytes 491524
Sparse Core Ops, SparseCore 0:
  184.5 7.4 reduce-scatter.1
where the time goes:
time: 372 us; the launch traced here: 366 us
  other arithmetic  137 us (37%)
  matrix products  95.2 us (26%)
  local copies, waits for them, and re-layouts  43.3 us (12%)
  blocking collectives  28.1 us (8%)
  starting transfers between devices  26.5 us (7%)
  waiting for transfers between devices  20 us (5%)
  between operations  15.3 us (4%)
    dot_general x8, matrix products, spectral_filter(): jnp.dot(coeffs * weights[None, :], fourier_basis.T, precision=lax.Precisi...  56.9 us
    cos x3, other arithmetic, spectral_filter(): jnp.cos(radians)  53.6 us
    unnamed x6, other arithmetic  42.2 us
    dot_general x8, matrix products, spectral_filter(): jnp.dot(rows_data, fourier_basis, precision=lax.Precision.HIGHEST, prefer...  38.3 us
    gather x3, local copies, waits for them, and re-layouts, per_device(): values = states[moment][0].reshape(-1)[local_index]  18.5 us
    scatter-add x3, other arithmetic, per_device(): jnp.zeros((tile_rows * tile_cols,), jnp.float32).at[local_index]  17.9 us
    sin x1, other arithmetic, spectral_filter(): jnp.sin(radians)  17.6 us
    unnamed x68, local copies, waits for them, and re-layouts  14.9 us
  transfers between devices with their start and end apart: 11, of which 6 were waited for; matrix products, arithmetic and copies ran while one was open for 23% of the time, Pallas kernels for 0%

commit v1 on v0

v1 whole, which is shorter than its diff:
```python
import math

import jax
import jax.numpy as jnp
import numpy as np
from jax import lax
from jax.sharding import PartitionSpec as P

COURANT = 0.4


def tables(parts, cols, waves):
    length = parts * cols
    inner_waves = waves // parts
    k1 = np.arange(parts)
    turn = 2 * np.pi * (np.outer(k1, np.arange(parts)) % parts) / parts
    outer = np.concatenate([np.cos(turn), -np.sin(turn)])
    twist = 2 * np.pi * np.outer(k1, np.arange(cols)) / length
    phase = 2 * np.pi * (np.outer(np.arange(cols), np.arange(inner_waves)) % cols) / cols
    c, s = np.cos(phase), np.sin(phase)
    inner = np.block([[c, -s], [s, c]])
    return [np.asarray(t, np.float32) for t in (outer, np.cos(twist), np.sin(twist), inner)]


def mul(a, b):
    return jnp.dot(a, b, precision=lax.Precision.HIGH, preferred_element_type=jnp.float32)


def spectral_filter(blocks, loc_spectrum):
    parts, items, cols = blocks.shape
    outer, tw_c, tw_s, inner = tables(parts, cols, loc_spectrum.shape[0])
    tw_c, tw_s = tw_c[:, None, :], tw_s[:, None, :]
    half = inner.shape[1] // 2
    weights = loc_spectrum.reshape(half, parts).T
    weights = jnp.concatenate([weights, weights], axis=1)[:, None, :]
    big = np.kron(outer, np.eye(items, dtype=np.float32))
    y = mul(big, blocks.astype(jnp.float32).reshape(parts * items, cols))
    y = y.reshape(2, parts, items, cols)
    y = jnp.concatenate([y[0] * tw_c + y[1] * tw_s, y[1] * tw_c - y[0] * tw_s], axis=2)
    z = mul(y.reshape(parts * items, 2 * cols), inner)
    z = (z.reshape(parts, items, 2 * half) * weights).reshape(parts * items, 2 * half)
    v = mul(z, inner.T).reshape(parts, items, 2, cols)
    re, im = v[:, :, 0], v[:, :, 1]
    v = jnp.stack([re * tw_c - im * tw_s, im * tw_c + re * tw_s])
    return mul(big.T, v.reshape(2 * parts * items, cols)).reshape(parts, items, cols)


def dx(q):
    return 0.5 * (jnp.roll(q, -1, axis=-1) - jnp.roll(q, 1, axis=-1))


def dy(q):
    padded = jnp.pad(q, ((1, 1), (0, 0)))
    return 0.5 * (padded[2:] - padded[:-2])


def model_step(state, rotation):
    h, u, w = state
    h = h - COURANT * (dx(u) + dy(w))
    return h, u - COURANT * dx(h) + rotation * w, w - COURANT * dy(h) - rotation * u


def adjoint_step(state, rotation):
    h, u, w = state
    a = h + COURANT * (dx(u) + dy(w))
    return a, u - rotation * w + COURANT * dx(a), w + rotation * u + COURANT * dy(a)


HALO = 8


def widen(block):
    count = lax.axis_size("sp")
    up = [(i, (i + 1) % count) for i in range(count)]
    down = [(b, a) for a, b in up]
    low = lax.ppermute(block[..., -HALO:], "sp", up)
    high = lax.ppermute(block[..., :HALO], "sp", down)
    return jnp.concatenate([low, block, high], axis=-1)


def split2(x):
    hi = x.astype(jnp.bfloat16)
    return hi, (x - hi.astype(jnp.float32)).astype(jnp.bfloat16)


def per_device(alpha, ensemble, static_std, control, loc_spectrum, obs_cell, obs_step, innovation, obs_weight):
    members, rows, cols = alpha.shape
    groups, parts = lax.axis_size("grp"), lax.axis_size("sp")
    spread = 1.0 / math.sqrt(members * groups - 1)
    tile_rows = control.shape[1]
    own = rows // parts
    first_row = lax.axis_index("grp") * tile_rows
    first_col = lax.axis_index("sp") * cols

    def localize(fields):
        sent = fields.astype(jnp.bfloat16).transpose(1, 0, 2)
        got = lax.all_to_all(sent, "sp", 0, 0, tiled=True)
        out = spectral_filter(got.reshape(parts, own * members, cols), loc_spectrum)
        out = out.astype(jnp.bfloat16).reshape(rows, members, cols)
        return lax.all_to_all(out, "sp", 0, 0, tiled=True).transpose(1, 0, 2)

    localized = localize(alpha).astype(jnp.float32)
    partial = jnp.sum(ensemble.astype(jnp.float32) * localized[:, None], axis=0)
    base = jnp.zeros((3, rows, cols), jnp.float32)
    base = lax.dynamic_update_slice(base, static_std * control, (0, first_row, 0))
    increment = lax.psum(base + spread * partial, "grp")
    rotation = (0.1 + 0.2 * (jnp.arange(rows, dtype=jnp.float32) + 0.5) / rows)[:, None]
    state0 = tuple(widen(increment))
    state1 = model_step(state0, rotation)
    state2 = model_step(state1, rotation)
    heights = jnp.stack([s[0] for s in (state0, state1, state2)])[..., HALO:-HALO]
    heights = lax.dynamic_slice_in_dim(heights, first_row, tile_rows, axis=1)
    heights = heights.reshape(3 * tile_rows, cols)
    row = obs_cell // (cols * parts) - first_row
    col = obs_cell % (cols * parts) - first_col
    in_col = (col[:, None] == jnp.arange(cols)).astype(jnp.bfloat16)
    in_row = (obs_step * tile_rows + row)[:, None] == jnp.arange(3 * tile_rows)
    picked = jnp.dot(in_col, jnp.concatenate(split2(heights)).T, preferred_element_type=jnp.float32)
    picked = picked[:, : 3 * tile_rows] + picked[:, 3 * tile_rows :]
    observed = jnp.sum(jnp.where(in_row, picked, 0.0), axis=1)
    misfit = obs_weight * (observed - innovation)
    placed = jnp.where(in_row, misfit[:, None], 0.0)
    forcing = jnp.dot(jnp.concatenate(split2(placed), axis=1).T, in_col, preferred_element_type=jnp.float32)
    forcing = (forcing[: 3 * tile_rows] + forcing[3 * tile_rows :]).reshape(3, tile_rows, cols)
    forcing = widen(lax.all_gather(forcing, "grp", axis=1, tiled=True))
    zero = jnp.zeros_like(forcing[0])
    h, u, w = adjoint_step((forcing[2], zero, zero), rotation)
    h, u, w = adjoint_step((h + forcing[1], u, w), rotation)
    adjoint = jnp.stack([h + forcing[0], u, w])[..., HALO:-HALO]
    tile = lax.dynamic_slice_in_dim(adjoint, first_row, tile_rows, axis=1)
    grad_control = control + static_std * tile
    half = adjoint.astype(jnp.bfloat16).astype(jnp.float32)
    weighted = jnp.sum(ensemble.astype(jnp.float32) * half[None], axis=1)
    grad_alpha = alpha + spread * localize(weighted).astype(jnp.float32)
    return grad_alpha, grad_control


def solution(mesh):
    flat = P(("grp", "sp"))
    tile = P(None, "grp", "sp")
    return jax.shard_map(
        per_device,
        mesh=mesh,
        in_specs=(P("grp", None, "sp"), P("grp", None, None, "sp"), tile, tile, P(), flat, flat, flat, flat),
        out_specs=(P("grp", None, "sp"), tile),
        check_vma=False,
    )
```

time: 372 us -> 94.1 us (0.25); the launches traced: 366 us -> 93.3 us
  other arithmetic: 137 us -> 3.23 us
  matrix products: 95.2 us -> 3.1 us
  local copies, waits for them, and re-layouts: 43.3 us -> 12 us
  between operations: 15.3 us -> 1.17 us
    dot_general x16 -> x10, matrix products: 95.2 us -> 3.1 us  [the longest x8 2.38 us: mul(): jnp.dot(a, b, precision=lax.Precision.HIGH, preferred_element_type=jnp.fl...]
    cos x3 -> x0, other arithmetic: 53.6 us -> none  [spectral_filter(): jnp.cos(radians)]
    unnamed x6 -> x0, other arithmetic: 42.2 us -> none
    gather x3 -> x0, local copies, waits for them, and re-layouts: 18.5 us -> none  [per_device(): values = states[moment][0].reshape(-1)[local_index]]
    scatter-add x4 -> x0, other arithmetic: 17.9 us -> none  [the longest x3 17.9 us: per_device(): jnp.zeros((tile_rows * tile_cols,), jnp.float32).at[local_index]]
    sin x1 -> x0, other arithmetic: 17.6 us -> none  [spectral_filter(): jnp.sin(radians)]
    all_to_all x2 -> x3, waiting for transfers between devices: 7.04 us -> 20.6 us  [the longest x2 15.1 us: localize(): return lax.all_to_all(out, 'sp', 0, 0, tiled=True).transpose(1, 0, 2)]
    all_to_all x2 -> x1, blocking collectives: 23.7 us -> 13.5 us  [localize(): got = lax.all_to_all(sent, 'sp', 0, 0, tiled=True)]
  transfers between devices with their start and end apart: 11 -> 7, of which waited for: 6 -> 5; matrix products, arithmetic and copies ran while one was open for 23% -> 1% of each run, Pallas kernels for 0% -> 0%
where the time goes in v1:
time: 94.1 us; the launch traced here: 93.3 us
  blocking collectives  26.7 us (28%)
  starting transfers between devices  23.6 us (25%)
  waiting for transfers between devices  23.5 us (25%)
  local copies, waits for them, and re-layouts  12 us (13%)
  other arithmetic  3.23 us (3%)
  matrix products  3.1 us (3%)
  between operations  1.17 us (1%)
    all_to_all x2, waiting for transfers between devices, localize(): return lax.all_to_all(out, 'sp', 0, 0, tiled=True).transpose(1, 0, 2)  15.1 us
    all_to_all x1, blocking collectives, localize(): got = lax.all_to_all(sent, 'sp', 0, 0, tiled=True)  13.5 us
    ppermute x2, starting transfers between devices, widen(): high = lax.ppermute(block[..., :HALO], 'sp', down)  8.88 us
    psum x1, blocking collectives, per_device(): increment = lax.psum(base + spread * partial, 'grp')  8.65 us
    unnamed x33, local copies, waits for them, and re-layouts  7.9 us
    all_to_all x1, starting transfers between devices, localize(): got = lax.all_to_all(sent, 'sp', 0, 0, tiled=True)  7.52 us
    all_to_all x2, starting transfers between devices, localize(): return lax.all_to_all(out, 'sp', 0, 0, tiled=True).transpose(1, 0, 2)  7.16 us
    all_to_all x1, waiting for transfers between devices, localize(): got = lax.all_to_all(sent, 'sp', 0, 0, tiled=True)  5.51 us
  transfers between devices with their start and end apart: 7, of which 5 were waited for; matrix products, arithmetic and copies ran while one was open for 1% of the time, Pallas kernels for 0%

profile of v1, /device:TPU:0, one launch (start us, length us, event | category | flops | bytes accessed | tf_op | source)
XLA Modules:
  0.0 93.3 jit_solution(1954184808317779153)
XLA Ops:
  0.6 0.9 convert_bitcast_fusion.2
  1.6 0.7 copy.66
  2.3 7.5 %all-to-all-start = ((bf16[16,10,256]{2,1,0:T(8,128)(2,1)}), bf16[16,10,256]{2,1,0:T(8,128)(2,1)S(1)}, u32[]{:S(2)}, u32[]{:S(2)}) async-start(bf16[16,10,256]{2,1,0:T(8,128)(2,1)} %copy.66), calls=%async_computation | async-start | bytes 262144 | tf_op jit(solution)/shard_map/all_to_all | solution.py:97
  9.8 0.7 copy-done.7
  10.6 0.7 copy-done.8
  11.3 0.6 copy-done.13
  12.1 0.1 pad_maximum_fusion.6
  12.2 5.5 %all-to-all-done = bf16[16,10,256]{2,1,0:T(8,128)(2,1)S(1)} async-done(((bf16[16,10,256]{2,1,0:T(8,128)(2,1)}), bf16[16,10,256]{2,1,0:T(8,128)(2,1)S(1)}, u32[]{:S(2)}, u32[]{:S(2)}) %all-to-all-start) | async-done | bytes 81952 | tf_op jit(solution)/shard_map/all_to_all | solution.py:97
  17.7 0.2 fusion.94
  18.1 0.9 copy-done.1
  19.0 0.4 fusion
  19.4 0.6 copy-done.6
  20.0 0.3 fusion.23
  20.4 0.2 copy.71
  20.6 0.9 copy-done.3
  21.5 0.3 fusion.1
  21.8 0.7 convert_element_type.81
  22.5 3.5 %all-to-all-start.1 = ((bf16[16,10,256]{2,1,0:T(8,128)(2,1)}), bf16[16,10,256]{2,1,0:T(8,128)(2,1)S(1)}, u32[]{:S(2)}, u32[]{:S(2)}) async-start(bf16[16,10,256]{2,1,0:T(8,128)(2,1)} %convert_element_type.81), calls=%async_computation.1 | async-start | bytes 262144 | tf_op jit(solution)/shard_map/all_to_all | solution.py:100
  26.0 7.8 %all-to-all-done.1 = bf16[16,10,256]{2,1,0:T(8,128)(2,1)S(1)} async-done(((bf16[16,10,256]{2,1,0:T(8,128)(2,1)}), bf16[16,10,256]{2,1,0:T(8,128)(2,1)S(1)}, u32[]{:S(2)}, u32[]{:S(2)}) %all-to-all-start.1) | async-done | bytes 81952 | tf_op jit(solution)/shard_map/all_to_all | solution.py:100
  33.9 0.1 copy.72
  34.0 0.8 copy-done.2
  34.9 0.7 copy-done.9
  35.7 8.6 %psum.7 = f32[3,16,256]{2,1,0:T(8,128)S(1)} all-reduce(f32[3,16,256]{2,1,0:T(8,128)S(1)} %add_dynamic-update-slice_fusion), channel_id=1, replica_groups=mesh['grp'=2,'sp'=16] {'grp'}, use_global_device_ids=true, to_apply=%region_1.0 | all-reduce | flops 12288 | bytes 98304 | tf_op jit(solution)/shard_map/psum | solution.py:106
  44.3 0.1 fusion.81
  44.4 4.4 %collective-permute-start.1 = (f32[3,16,8]{2,1,0:T(8,128)S(1)}, f32[3,16,8]{2,1,0:T(8,128)S(1)}, u32[]{:S(2)}, u32[]{:S(2)}) collective-permute-start(f32[3,16,8]{2,1,0:T(8,128)S(1)} %get-tuple-element.34), channel_id=1, source_target_pairs={{1,0},{2,1},{3,2},{4,3},{5,4},{6,5},{7,6},{8,7},{9,8},{10,9},{11,1... | collective-permute-start | bytes 4616 | tf_op jit(solution)/shard_map/ppermute | solution.py:77
  48.9 1.5 %collective-permute-done = f32[3,16,8]{2,1,0:T(8,128)S(1)} collective-permute-done((f32[3,16,8]{2,1,0:T(8,128)S(1)}, f32[3,16,8]{2,1,0:T(8,128)S(1)}, u32[]{:S(2)}, u32[]{:S(2)}) %collective-permute-start) | collective-permute-done | bytes 1568 | tf_op jit(solution)/shard_map/ppermute | solution.py:76
  50.4 0.1 pad_maximum_fusion.2
  50.5 0.1 fusion.93
  50.6 0.1 fusion.29
  50.7 0.1 fusion.91
  50.9 0.1 fusion.60
  50.9 0.1 fusion.89
  51.1 0.1 fusion.38
  51.2 0.1 subtract_convert_fusion
  51.3 0.4 fusion.4
  51.7 0.6 copy-done.14
  52.4 0.4 fusion.3
  52.8 4.5 %all_gather.3 = f32[3,16,256]{2,1,0:T(8,128)S(1)} all-gather(f32[3,8,256]{2,1,0:T(8,128)S(1)} %fusion.57), channel_id=1, replica_groups=mesh['grp'=2,'sp'=16] {'grp'}, dimensions={1}, use_global_device_ids=true | all-gather | bytes 73728 | tf_op jit(solution)/shard_map/all_gather | solution.py:125
  57.3 0.1 fusion.80
  57.3 4.4 %collective-permute-start.3 = (f32[3,16,8]{2,1,0:T(8,128)S(1)}, f32[3,16,8]{2,1,0:T(8,128)S(1)}, u32[]{:S(2)}, u32[]{:S(2)}) collective-permute-start(f32[3,16,8]{2,1,0:T(8,128)S(1)} %get-tuple-element.32), channel_id=1, source_target_pairs={{1,0},{2,1},{3,2},{4,3},{5,4},{6,5},{7,6},{8,7},{9,8},{10,9},{11,1... | collective-permute-start | bytes 4616 | tf_op jit(solution)/shard_map/ppermute | solution.py:77
  61.8 0.1 fusion.74
  61.9 1.4 %collective-permute-done.2 = f32[3,16,8]{2,1,0:T(8,128)S(1)} collective-permute-done((f32[3,16,8]{2,1,0:T(8,128)S(1)}, f32[3,16,8]{2,1,0:T(8,128)S(1)}, u32[]{:S(2)}, u32[]{:S(2)}) %collective-permute-start.2) | collective-permute-done | bytes 1568 | tf_op jit(solution)/shard_map/ppermute | solution.py:76
  63.3 0.1 pad_maximum_fusion.3
  63.4 0.1 fusion.56
  63.5 0.1 fusion.87
  63.6 0.1 fusion.41
  63.7 0.1 fusion.84
  63.9 0.1 fusion.54
  64.0 0.1 fusion.83
  64.1 0.1 fusion.68
  64.2 0.1 convert_convert_fusion
  64.4 13.5 %all_to_all.20 = bf16[16,10,256]{2,1,0:T(8,128)(2,1)S(1)} all-to-all(bf16[16,10,256]{2,1,0:T(8,128)(2,1)S(1)} %copy.73), channel_id=1, replica_groups=mesh['grp'=2,'sp'=16] {'sp'}, dimensions={0} | all-to-all | bytes 163840 | tf_op jit(solution)/shard_map/all_to_all | solution.py:97
  77.9 0.2 fusion.95
  78.3 0.4 convolution_multiply_fusion
  78.7 0.5 copy-done.5
  79.2 0.3 fusion.21
  79.6 0.2 copy.77
  79.9 0.3 fusion.2
  80.2 0.7 convert_element_type.96
  80.9 3.6 %all-to-all-start.3 = ((bf16[16,10,256]{2,1,0:T(8,128)(2,1)}), bf16[16,10,256]{2,1,0:T(8,128)(2,1)S(1)}, u32[]{:S(2)}, u32[]{:S(2)}) async-start(bf16[16,10,256]{2,1,0:T(8,128)(2,1)} %convert_element_type.96), calls=%async_computation.3 | async-start | bytes 262144 | tf_op jit(solution)/shard_map/all_to_all | solution.py:100
  84.5 0.6 multiply_add_fusion.4
  85.1 7.2 %all-to-all-done.3 = bf16[16,10,256]{2,1,0:T(8,128)(2,1)S(1)} async-done(((bf16[16,10,256]{2,1,0:T(8,128)(2,1)}), bf16[16,10,256]{2,1,0:T(8,128)(2,1)S(1)}, u32[]{:S(2)}, u32[]{:S(2)}) %all-to-all-start.3) | async-done | bytes 81952 | tf_op jit(solution)/shard_map/all_to_all | solution.py:100
  92.4 0.1 bitcast_add_fusion
  92.5 0.8 copy.79
  (71 shorter events, 1.6 us)
Async XLA Ops:
  2.2 7.5 %copy-start.11 = (s32[1024]{0:T(1024)S(1)}, s32[1024]{0:T(1024)}, u32[]{:S(2)}) copy-start(s32[1024]{0:T(1024)} %param.27) | copy-start | bytes 12292
  2.2 7.6 %copy-start.12 = (s32[1024]{0:T(1024)S(1)}, s32[1024]{0:T(1024)}, u32[]{:S(2)}) copy-start(s32[1024]{0:T(1024)} %param.26) | copy-start | bytes 12292
  2.3 15.4 %all-to-all-start = ((bf16[16,10,256]{2,1,0:T(8,128)(2,1)}), bf16[16,10,256]{2,1,0:T(8,128)(2,1)S(1)}, u32[]{:S(2)}, u32[]{:S(2)}) async-start(bf16[16,10,256]{2,1,0:T(8,128)(2,1)} %copy.66), calls=%async_computation | async-start | bytes 262144 | tf_op jit(solution)/shard_map/all_to_all | solution.py:97
  9.8 0.7 copy-start.7
  10.5 0.7 copy-start.8
  11.3 0.7 copy-start.13
  11.3 6.4 %copy-start = (f32[320,160]{1,0:T(8,128)S(1)}, f32[320,160]{1,0:T(8,128)}, u32[]{:S(2)}) copy-start(f32[320,160]{1,0:T(8,128)} %constant.90.clone) | copy-start | bytes 614404
  18.1 1.0 %copy-start.1 = (f32[512,128,1]{1,0,2:T(8,128)S(1)}, f32[512,128,1]{1,0,2:T(8,128)}, u32[]{:S(2)}) copy-start(f32[512,128,1]{1,0,2:T(8,128)} %constant.116) | copy-start | bytes 786436
  19.0 0.9 %copy-start.6 = (f32[2,256,128,1]{2,1,0,3:T(8,128)S(1)}, f32[2,256,128,1]{2,1,0,3:T(8,128)}, u32[]{:S(2)}) copy-start(f32[2,256,128,1]{2,1,0,3:T(8,128)} %constant.117) | copy-start | bytes 786436
  20.6 0.9 %copy-start.3 = (f32[160,320]{1,0:T(8,128)S(1)}, f32[160,320]{1,0:T(8,128)}, u32[]{:S(2)}) copy-start(f32[160,320]{1,0:T(8,128)} %constant.95.clone) | copy-start | bytes 614404
  22.5 11.4 %all-to-all-start.1 = ((bf16[16,10,256]{2,1,0:T(8,128)(2,1)}), bf16[16,10,256]{2,1,0:T(8,128)(2,1)S(1)}, u32[]{:S(2)}, u32[]{:S(2)}) async-start(bf16[16,10,256]{2,1,0:T(8,128)(2,1)} %convert_element_type.81), calls=%async_computation.1 | async-start | bytes 262144 | tf_op jit(solution)/shard_map/all_to_all | solution.py:100
  33.9 0.9 %copy-start.2 = (bf16[10,3,16,256]{3,2,1,0:T(8,128)(2,1)S(1)}, bf16[10,3,16,256]{3,2,1,0:T(8,128)(2,1)}, u32[]{:S(2)}) copy-start(bf16[10,3,16,256]{3,2,1,0:T(8,128)(2,1)} %param.22) | copy-start | bytes 737284
  34.9 0.7 copy-start.9
  34.9 0.7 copy-start.10
  44.4 6.0 %collective-permute-start = (f32[3,16,8]{2,1,0:T(8,128)S(1)}, f32[3,16,8]{2,1,0:T(8,128)S(1)}, u32[]{:S(2)}, u32[]{:S(2)}) collective-permute-start(f32[3,16,8]{2,1,0:T(8,128)S(1)} %get-tuple-element.33), channel_id=1, source_target_pairs={{0,1},{1,2},{2,3},{3,4},{4,5},{5,6},{6,7},{7,8},{8,9},{9,10},{10,1... | collective-permute-start | bytes 4616 | tf_op jit(solution)/shard_map/ppermute | solution.py:76
  44.4 6.0 %collective-permute-start.1 = (f32[3,16,8]{2,1,0:T(8,128)S(1)}, f32[3,16,8]{2,1,0:T(8,128)S(1)}, u32[]{:S(2)}, u32[]{:S(2)}) collective-permute-start(f32[3,16,8]{2,1,0:T(8,128)S(1)} %get-tuple-element.34), channel_id=1, source_target_pairs={{1,0},{2,1},{3,2},{4,3},{5,4},{6,5},{7,6},{8,7},{9,8},{10,9},{11,1... | collective-permute-start | bytes 4616 | tf_op jit(solution)/shard_map/ppermute | solution.py:77
  51.6 0.7 copy-start.14
  51.6 0.7 copy-start.15
  57.3 6.0 %collective-permute-start.2 = (f32[3,16,8]{2,1,0:T(8,128)S(1)}, f32[3,16,8]{2,1,0:T(8,128)S(1)}, u32[]{:S(2)}, u32[]{:S(2)}) collective-permute-start(f32[3,16,8]{2,1,0:T(8,128)S(1)} %get-tuple-element.31), channel_id=1, source_target_pairs={{0,1},{1,2},{2,3},{3,4},{4,5},{5,6},{6,7},{7,8},{8,9},{9,10},{10,1... | collective-permute-start | bytes 4616 | tf_op jit(solution)/shard_map/ppermute | solution.py:76
  57.3 6.0 %collective-permute-start.3 = (f32[3,16,8]{2,1,0:T(8,128)S(1)}, f32[3,16,8]{2,1,0:T(8,128)S(1)}, u32[]{:S(2)}, u32[]{:S(2)}) collective-permute-start(f32[3,16,8]{2,1,0:T(8,128)S(1)} %get-tuple-element.32), channel_id=1, source_target_pairs={{1,0},{2,1},{3,2},{4,3},{5,4},{6,5},{7,6},{8,7},{9,8},{10,9},{11,1... | collective-permute-start | bytes 4616 | tf_op jit(solution)/shard_map/ppermute | solution.py:77
  78.3 1.0 %copy-start.5 = (f32[2,256,128,1]{2,1,3,0:T(8,128)S(1)}, f32[2,256,128,1]{2,1,3,0:T(8,128)}, u32[]{:S(2)}) copy-start(f32[2,256,128,1]{2,1,3,0:T(8,128)} %constant.118) | copy-start | bytes 786436
  80.9 11.5 %copy-start.4 = (f32[10,16,256]{2,1,0:T(8,128)S(1)}, f32[10,16,256]{2,1,0:T(8,128)}, u32[]{:S(2)}) copy-start(f32[10,16,256]{2,1,0:T(8,128)} %param.21) | copy-start | bytes 491524
  80.9 11.5 %all-to-all-start.3 = ((bf16[16,10,256]{2,1,0:T(8,128)(2,1)}), bf16[16,10,256]{2,1,0:T(8,128)(2,1)S(1)}, u32[]{:S(2)}, u32[]{:S(2)}) async-start(bf16[16,10,256]{2,1,0:T(8,128)(2,1)} %convert_element_type.96), calls=%async_computation.3 | async-start | bytes 262144 | tf_op jit(solution)/shard_map/all_to_all | solution.py:100

commit v2 on v1

v2 whole, which is shorter than its diff:
```python
import functools
import math

import jax
import jax.numpy as jnp
import numpy as np
from jax import lax
from jax.experimental import pallas as pl
from jax.experimental.pallas import tpu as pltpu
from jax.sharding import PartitionSpec as P

COURANT = 0.4


def tables(parts, cols, waves):
    length = parts * cols
    inner_waves = waves // parts
    k1 = np.arange(parts)
    turn = 2 * np.pi * (np.outer(k1, np.arange(parts)) % parts) / parts
    outer = np.concatenate([np.cos(turn), -np.sin(turn)])
    twist = 2 * np.pi * np.outer(k1, np.arange(cols)) / length
    phase = 2 * np.pi * (np.outer(np.arange(cols), np.arange(inner_waves)) % cols) / cols
    c, s = np.cos(phase), np.sin(phase)
    inner = np.block([[c, -s], [s, c]])
    return [np.asarray(t, np.float32) for t in (outer, np.cos(twist), np.sin(twist), inner)]


EDGE = 128
BF16, F32 = jnp.bfloat16, jnp.float32


def dot(a, b, contract=((1,), (0,))):
    return lax.dot_general(a, b, (contract, ((), ())), preferred_element_type=F32)


def split2(x):
    hi = x.astype(BF16)
    return hi, (x - hi.astype(F32)).astype(BF16)


def right_mul(x, hi, lo):
    x_hi, x_lo = split2(x)
    return dot(x_hi, hi) + dot(x_lo, hi) + dot(x_hi, lo)


def left_mul(hi, lo, x):
    x_hi, x_lo = split2(x)
    return dot(hi, x_hi) + dot(hi, x_lo) + dot(lo, x_hi)


def dx(q):
    width = q.shape[1]
    return 0.5 * (pltpu.roll(q, width - 1, 1) - pltpu.roll(q, 1, 1))


def dy(q):
    rows = q.shape[0]
    at = lax.broadcasted_iota(jnp.int32, q.shape, 0)
    above = jnp.where(at < rows - 1, pltpu.roll(q, rows - 1, 0), 0.0)
    below = jnp.where(at > 0, pltpu.roll(q, 1, 0), 0.0)
    return 0.5 * (above - below)


def model_step(state, rotation):
    h, u, w = state
    h = h - COURANT * (dx(u) + dy(w))
    return h, u - COURANT * dx(h) + rotation * w, w - COURANT * dy(h) - rotation * u


def adjoint_step(state, rotation):
    h, u, w = state
    a = h + COURANT * (dx(u) + dy(w))
    return a, u - rotation * w + COURANT * dx(a), w + rotation * u + COURANT * dy(a)


def kernel(
    groups, parts, spread,
    alpha_ref, ens_ref, base_ref, weights_ref, tw_c_ref, tw_s_ref,
    big_hi, big_lo, bigt_hi, bigt_lo, in_hi, in_lo, int_hi, int_lo,
    col_ref, slot_ref, innovation_ref, obs_weight_ref,
    filtered_ref, adjoint_ref,
    snd, rcv, ex_src, ex_full, ex_low, ex_high,
    send_sem, recv_sem, ex_send, ex_recv,
):
    group, part = lax.axis_index("grp"), lax.axis_index("sp")
    left, right = lax.rem(part + parts - 1, parts), lax.rem(part + 1, parts)
    _, rows, cols = base_ref.shape
    own, padded = rows // parts, alpha_ref.shape[2]
    items = parts * own * padded

    barrier = pltpu.get_barrier_semaphore()
    for i in range(1, parts):
        pl.semaphore_signal(barrier, inc=1, device_id={"sp": lax.rem(part + i, parts)})
    for i in range(1, groups):
        for at in (left, part, right):
            pl.semaphore_signal(barrier, inc=1, device_id={"grp": lax.rem(group + i, groups), "sp": at})
    pl.semaphore_wait(barrier, parts - 1 + 3 * (groups - 1))

    def all_to_all(phase, source):
        copies = []
        for i in range(1, parts):
            to = lax.rem(part + i, parts)
            copies.append(pltpu.make_async_remote_copy(
                src_ref=source.at[to], dst_ref=rcv.at[phase, part],
                send_sem=send_sem.at[phase, i], recv_sem=recv_sem.at[phase, i],
                device_id={"sp": to},
            ))
            copies[-1].start()
        rcv[phase, part] = source[part]
        return copies

    def finish(copies):
        for copy in copies:
            copy.wait_recv()
        for copy in copies:
            copy.wait_send()

    def filtered(phase):
        x = rcv[phase].reshape(items, cols)
        c, s = tw_c_ref[...], tw_s_ref[...]
        y = dot(big_hi[...], x) + dot(big_lo[...], x)
        re, im = y[:items], y[items:]
        z = right_mul(re * c + im * s, in_hi[:cols], in_lo[:cols])
        z = z + right_mul(im * c - re * s, in_hi[cols:], in_lo[cols:])
        v = right_mul(z * weights_ref[...], int_hi[...], int_lo[...])
        re, im = v[:, :cols], v[:, cols:]
        out = left_mul(bigt_hi[:, :items], bigt_lo[:, :items], re * c - im * s)
        out = out + left_mul(bigt_hi[:, items:], bigt_lo[:, items:], im * c + re * s)
        return out.astype(BF16).reshape(parts, own, padded, cols)

    def exchange(step, fields):
        for v in range(3):
            ex_src[step, v] = fields[v]
        copies = []
        first, last = pl.ds(0, EDGE), pl.ds(cols - EDGE, EDGE)
        for i in range(groups):
            to = lax.rem(group + i, groups)
            plans = [(1, right, ex_src.at[step, :, :, last], ex_low), (2, left, ex_src.at[step, :, :, first], ex_high)]
            if i > 0:
                plans.append((0, part, ex_src.at[step], ex_full))
            for kind, at, source, target in plans:
                copies.append(pltpu.make_async_remote_copy(
                    src_ref=source, dst_ref=target.at[step, group],
                    send_sem=ex_send.at[step, kind, i], recv_sem=ex_recv.at[step, kind, i],
                    device_id={"grp": to, "sp": at},
                ))
                copies[-1].start()
        ex_full[step, group] = ex_src[step]
        finish(copies)
        wide = []
        for v in range(3):
            pieces = []
            for buffer in (ex_low, ex_full, ex_high):
                total = buffer[step, 0, v]
                for g in range(1, groups):
                    total = total + buffer[step, g, v]
                pieces.append(total)
            wide.append(jnp.concatenate(pieces, axis=1))
        return wide

    copies = all_to_all(0, alpha_ref)
    in_col = (lax.broadcasted_iota(jnp.int32, (cols, col_ref.shape[1]), 0) == col_ref[...]).astype(F32).astype(BF16)
    in_slot = lax.broadcasted_iota(jnp.int32, (3 * rows, col_ref.shape[1]), 0) == slot_ref[...]
    finish(copies)
    snd[0] = filtered(0)
    finish(all_to_all(1, snd.at[0]))
    localized = rcv[1].reshape(rows, padded, cols).astype(F32)
    partial = [base_ref[v] + spread * jnp.sum(ens_ref[v].astype(F32) * localized, axis=1) for v in range(3)]
    state0 = exchange(0, partial)
    row_at = lax.broadcasted_iota(jnp.int32, (rows, cols + 2 * EDGE), 0).astype(F32)
    rotation = 0.1 + 0.2 * (row_at + 0.5) / rows
    state1 = model_step(state0, rotation)
    state2 = model_step(state1, rotation)
    heights = jnp.concatenate([s[0][:, EDGE:-EDGE] for s in (state0, state1, state2)], axis=0)
    high, low = split2(heights)
    picked = dot(high, in_col) + dot(low, in_col)
    observed = jnp.sum(jnp.where(in_slot, picked, 0.0), axis=0, keepdims=True)
    misfit = obs_weight_ref[...] * (observed - innovation_ref[...])
    high, low = split2(jnp.where(in_slot, misfit, 0.0))
    forcing = dot(high, in_col, ((1,), (1,))) + dot(low, in_col, ((1,), (1,)))
    forcing = exchange(1, [forcing[t * rows : (t + 1) * rows] for t in range(3)])
    zero = jnp.zeros_like(rotation)
    h, u, w = adjoint_step((forcing[2], zero, zero), rotation)
    h, u, w = adjoint_step((h + forcing[1], u, w), rotation)
    weighted = jnp.zeros((rows, padded, cols), F32)
    for v, field in enumerate((h + forcing[0], u, w)):
        field = field[:, EDGE:-EDGE]
        adjoint_ref[v] = field
        half = field.astype(BF16).astype(F32)
        weighted = weighted + ens_ref[v].astype(F32) * half[:, None, :]
    snd[1] = weighted.astype(BF16).reshape(parts, own, padded, cols)
    finish(all_to_all(2, snd.at[1]))
    snd[2] = filtered(2)
    finish(all_to_all(3, snd.at[2]))
    filtered_ref[...] = rcv[3].reshape(rows, padded, cols)


def both(table):
    hi = table.astype(BF16)
    return hi, (table - hi.astype(np.float32)).astype(BF16)


def per_device(alpha, ensemble, static_std, control, loc_spectrum, obs_cell, obs_step, innovation, obs_weight):
    members, rows, cols = alpha.shape
    groups, parts = lax.axis_size("grp"), lax.axis_size("sp")
    spread = 1.0 / math.sqrt(members * groups - 1)
    tile_rows, own = control.shape[1], rows // parts
    padded = -(-members // 16) * 16
    first_row = lax.axis_index("grp") * tile_rows
    first_col = lax.axis_index("sp") * cols
    fill = padded - members

    outer, tw_c, tw_s, inner = tables(parts, cols, loc_spectrum.shape[0])
    items = own * padded
    big = np.kron(outer, np.eye(items, dtype=np.float32))
    waves = loc_spectrum.reshape(inner.shape[1] // 2, parts).T
    waves = jnp.repeat(jnp.concatenate([waves, waves], axis=1), items, axis=0)
    sent = jnp.pad(alpha.astype(BF16).transpose(1, 0, 2), ((0, 0), (0, fill), (0, 0)))
    ens = jnp.pad(ensemble.transpose(1, 2, 0, 3), ((0, 0), (0, 0), (0, fill), (0, 0)))
    base = jnp.zeros((3, rows, cols), F32)
    base = lax.dynamic_update_slice(base, static_std * control, (0, first_row, 0))
    col = obs_cell % (cols * parts) - first_col
    slot = obs_step * rows + obs_cell // (cols * parts)
    vmem = pl.BlockSpec(memory_space=pltpu.VMEM)
    operands = (
        sent.reshape(parts, own, padded, cols), ens, base, waves,
        np.repeat(tw_c, items, axis=0), np.repeat(tw_s, items, axis=0),
        *both(big), *both(big.T), *both(inner), *both(inner.T),
        col[None], slot[None], innovation[None], obs_weight[None],
    )
    filtered, adjoint = pl.pallas_call(
        functools.partial(kernel, groups, parts, spread),
        out_shape=(
            jax.ShapeDtypeStruct((rows, padded, cols), BF16),
            jax.ShapeDtypeStruct((3, rows, cols), F32),
        ),
        in_specs=[vmem] * len(operands),
        out_specs=(vmem, vmem),
        scratch_shapes=[
            pltpu.VMEM((3, parts, own, padded, cols), BF16),
            pltpu.VMEM((4, parts, own, padded, cols), BF16),
            pltpu.VMEM((2, 3, rows, cols), F32),
            pltpu.VMEM((2, groups, 3, rows, cols), F32),
            pltpu.VMEM((2, groups, 3, rows, EDGE), F32),
            pltpu.VMEM((2, groups, 3, rows, EDGE), F32),
            pltpu.SemaphoreType.DMA((4, parts)),
            pltpu.SemaphoreType.DMA((4, parts)),
            pltpu.SemaphoreType.DMA((2, 3, groups)),
            pltpu.SemaphoreType.DMA((2, 3, groups)),
        ],
        compiler_params=pltpu.CompilerParams(collective_id=0, has_side_effects=True, vmem_limit_bytes=60 << 20),
    )(*operands)
    filtered = filtered[:, :members].transpose(1, 0, 2).astype(F32)
    grad_alpha = alpha + spread * filtered
    tile = lax.dynamic_slice_in_dim(adjoint, first_row, tile_rows, axis=1)
    return grad_alpha, control + static_std * tile


def solution(mesh):
    flat = P(("grp", "sp"))
    tile = P(None, "grp", "sp")
    return jax.shard_map(
        per_device,
        mesh=mesh,
        in_specs=(P("grp", None, "sp"), P("grp", None, None, "sp"), tile, tile, P(), flat, flat, flat, flat),
        out_specs=(P("grp", None, "sp"), tile),
        check_vma=False,
    )
```

time: 94.1 us -> 52.3 us (0.56)
  Pallas kernels: 0 us -> 42.4 us
  blocking collectives: 26.7 us -> 0 us
  starting transfers between devices: 23.6 us -> 0 us
  waiting for transfers between devices: 23.5 us -> 0 us
  local copies, waits for them, and re-layouts: 12 us -> 5.69 us
  matrix products: 3.1 us -> 0 us
    pallas_call x0 -> x1, Pallas kernels: none -> 42.4 us  [per_device(): pl.pallas_call(functools.partial(kernel, groups, parts, spread), out_shap...]
    all_to_all x3 -> x0, waiting for transfers between devices: 20.6 us -> none  [the longest x2 15.1 us: localize(): return lax.all_to_all(out, 'sp', 0, 0, tiled=True).transpose(1, 0, 2)]
    all_to_all x3 -> x0, starting transfers between devices: 14.7 us -> none  [the longest x1 7.52 us: localize(): got = lax.all_to_all(sent, 'sp', 0, 0, tiled=True)]
    all_to_all x1 -> x0, blocking collectives: 13.5 us -> none  [localize(): got = lax.all_to_all(sent, 'sp', 0, 0, tiled=True)]
    ppermute x4 -> x0, starting transfers between devices: 8.88 us -> none  [the longest x2 8.88 us: widen(): high = lax.ppermute(block[..., :HALO], 'sp', down)]
    psum x1 -> x0, blocking collectives: 8.65 us -> none  [per_device(): increment = lax.psum(base + spread * partial, 'grp')]
    unnamed x33 -> x16, local copies, waits for them, and re-layouts: 7.9 us -> 3.39 us
    all_gather x1 -> x0, blocking collectives: 4.5 us -> none  [per_device(): forcing = widen(lax.all_gather(forcing, 'grp', axis=1, tiled=True))]
  transfers between devices with their start and end apart: 7 -> 0, of which waited for: 5 -> 0; matrix products, arithmetic and copies ran while one was open for 1% -> 0% of each run, Pallas kernels for 0% -> 0%
where the time goes in v2:
time: 52.3 us; the launch traced here: 51.9 us
  Pallas kernels  42.4 us (81%)
  local copies, waits for them, and re-layouts  5.69 us (11%)
  other arithmetic  3.07 us (6%)
  between operations  0.73 us (1%)
    pallas_call x1, Pallas kernels, per_device(): pl.pallas_call(functools.partial(kernel, groups, parts, spread), out_shap...  42.4 us
    unnamed x16, local copies, waits for them, and re-layouts  3.39 us
    add x1, other arithmetic, per_device(): return (grad_alpha, control + static_std * tile)  1.36 us

profile of v2, /device:TPU:0, one launch (start us, length us, event | category | flops | bytes accessed | tf_op | source)
XLA Modules:
  0.0 51.9 jit_solution(8788866988161266593)
XLA Ops:
  0.6 0.0 copy-start.2
  0.6 0.0 copy-start.3
  0.7 0.7 %copy-done.2 = f32[3,8,256]{2,1,0:T(8,128)S(1)} copy-done((f32[3,8,256]{2,1,0:T(8,128)S(1)}, f32[3,8,256]{2,1,0:T(8,128)}, u32[]{:S(2)}) %copy-start.2) | copy-done | bytes 24600
  1.4 0.0 copy-done.3
  1.4 0.0 copy-start.6
  1.4 0.0 copy-start.1
  1.4 0.0 copy-start.5
  1.4 0.7 %copy-done.6 = s32[1024]{0:T(1024)S(1)} copy-done((s32[1024]{0:T(1024)S(1)}, s32[1024]{0:T(1024)}, u32[]{:S(2)}) %copy-start.6) | copy-done | bytes 4120
  2.1 0.0 copy-done.5
  2.1 0.6 %fusion.1 = (s32[1024]{0:T(1024)}, s32[1024]{0:T(1024)}) fusion(s32[1024]{0:T(1024)S(1)} %copy-done.5, s32[1024]{0:T(1024)S(1)} %copy-done.6, s32[]{:T(128)S(6)} %mul.29), kind=kLoop, calls=%fused_computation.13 | loop fusion | flops 22528 | bytes 16388 | tf_op jit(solution)/shard_map/add | solution.py:223
  2.7 1.0 %copy.45 = bf16[10,3,16,256]{3,0,2,1:T(8,128)(2,1)S(1)} copy(bf16[10,3,16,256]{3,2,1,0:T(8,128)(2,1)} %param.20) | data formatting | bytes 491520 | tf_op args[1]
  3.8 0.0 copy-done.1
  3.8 0.0 copy-start
  3.8 0.8 %pad.9.ens_ref = bf16[3,16,16,256]{3,2,1,0:T(8,128)(2,1)} pad(bf16[3,16,10,256]{3,2,1,0:T(8,128)(2,1)S(1)} %bitcast.16, bf16[]{:T(256)} %constant.56.clone.1), padding=0_0x0_0x0_6x0_0 | pad | bytes 638978 | tf_op jit(solution)/shard_map/jit(_pad)/pad | solution.py:219
  4.6 0.2 copy-done
  4.8 0.0 copy-start.4
  4.8 0.7 %pad_bitcast_fusion.alpha_ref = bf16[16,1,16,256]{3,2,1,0:T(8,128)(2,1)} fusion(bf16[16,10,256]{2,1,0:T(8,128)(2,1)S(1)} %bitcast.18), kind=kLoop, calls=%fused_computation.3 | loop fusion | bytes 212992 | tf_op jit(solution)/shard_map/reshape | solution.py:226
  5.4 0.0 copy-done.4
  5.4 0.1 reshape.14
  5.5 0.1 copy.38
  5.6 0.1 pad_maximum_fusion
  5.7 0.7 %broadcast_in_dim.19 = f32[16,16,128]{2,1,0:T(8,128)} broadcast(f32[16,128]{1,0:T(8,128)S(1)} %pad_maximum_fusion), dimensions={0,2} | broadcast | bytes 139264 | tf_op jit(solution)/shard_map/broadcast_in_dim | solution.py:217
  6.3 42.4 %shard_map.194 = (bf16[16,16,256]{2,1,0:T(8,128)(2,1)}, f32[3,16,256]{2,1,0:T(8,128)}) custom-call(bf16[16,1,16,256]{3,2,1,0:T(8,128)(2,1)} %pad_bitcast_fusion.alpha_ref, bf16[3,16,16,256]{3,2,1,0:T(8,128)(2,1)} %pad.9.ens_ref, f32[3,16,256]{2,1,0:T(8,128)} %copy-done.1, f32[256,128]{1,0:T(8,128)} %bitcast.17, f32[256,256]{1,0:T(8,128)} %constant.71.clone.tw_c_ref, ...), custom_call_target="tpu_custom_call" | custom-call | tf_op jit(solution)/shard_map/pallas_call | solution.py:231
  48.7 1.4 %multiply_add_fusion = f32[3,8,256]{2,1,0:T(8,128)} fusion(f32[3,8,256]{2,1,0:T(8,128)S(1)} %copy-done.3, f32[3,8,256]{2,1,0:T(8,128)S(1)} %copy-done.2, f32[3,16,256]{2,1,0:T(8,128)} %get-tuple-element.5, s32[]{:T(128)S(6)} %select_n.16), kind=kLoop, calls=%fused_computation.4 | loop fusion | flops 12288 | bytes 98308 | tf_op jit(solution)/shard_map/add | solution.py:256
  50.1 1.0 %bitcast_add_fusion = f32[10,16,256]{2,0,1:T(8,128)S(1)} fusion(f32[10,16,256]{2,1,0:T(8,128)S(1)} %copy-done, bf16[16,16,256]{2,1,0:T(8,128)(2,1)} %get-tuple-element.4), kind=kLoop, calls=%fused_computation.1 | loop fusion | flops 122880 | bytes 409600 | tf_op jit(solution)/shard_map/add | solution.py:254
  51.1 0.8 %copy.41 = f32[10,16,256]{2,1,0:T(8,128)} copy(f32[10,16,256]{2,0,1:T(8,128)S(1)} %bitcast_add_fusion) | data formatting | bytes 327680
  (4 shorter events, 0.1 us)
Async XLA Ops:
  0.6 0.7 %copy-start.2 = (f32[3,8,256]{2,1,0:T(8,128)S(1)}, f32[3,8,256]{2,1,0:T(8,128)}, u32[]{:S(2)}) copy-start(f32[3,8,256]{2,1,0:T(8,128)} %param.21) | copy-start | bytes 73732
  0.6 0.7 %copy-start.3 = (f32[3,8,256]{2,1,0:T(8,128)S(1)}, f32[3,8,256]{2,1,0:T(8,128)}, u32[]{:S(2)}) copy-start(f32[3,8,256]{2,1,0:T(8,128)} %param.22) | copy-start | bytes 73732
  1.4 0.7 %copy-start.6 = (s32[1024]{0:T(1024)S(1)}, s32[1024]{0:T(1024)}, u32[]{:S(2)}) copy-start(s32[1024]{0:T(1024)} %param.24) | copy-start | bytes 12292
  1.4 2.4 %copy-start.1 = (f32[3,16,256]{2,1,0:T(8,128)}, f32[3,16,256]{2,1,0:T(8,128)S(1)}, u32[]{:S(2)}) copy-start(f32[3,16,256]{2,1,0:T(8,128)S(1)} %multiply_dynamic-update-slice_fusion.base_ref) | copy-start | bytes 147460
  1.4 0.7 %copy-start.5 = (s32[1024]{0:T(1024)S(1)}, s32[1024]{0:T(1024)}, u32[]{:S(2)}) copy-start(s32[1024]{0:T(1024)} %param.25) | copy-start | bytes 12292
  3.8 0.9 %copy-start = (f32[10,16,256]{2,1,0:T(8,128)S(1)}, f32[10,16,256]{2,1,0:T(8,128)}, u32[]{:S(2)}) copy-start(f32[10,16,256]{2,1,0:T(8,128)} %param.19) | copy-start | bytes 491524
  4.8 0.7 %copy-start.4 = (f32[1024]{0:T(1024)S(1)}, f32[1024]{0:T(1024)}, u32[]{:S(2)}) copy-start(f32[1024]{0:T(1024)} %param.23) | copy-start | bytes 12292

commit v3 on v2

--- a/solution.py
+++ b/solution.py
@@ -75,17 +75,19 @@
 
 def kernel(
     groups, parts, spread,
-    alpha_ref, ens_ref, base_ref, weights_ref, tw_c_ref, tw_s_ref,
+    alpha_ref, ensemble_ref, std_ref, control_ref, weights_ref, tw_c_ref, tw_s_ref,
     big_hi, big_lo, bigt_hi, bigt_lo, in_hi, in_lo, int_hi, int_lo,
-    col_ref, slot_ref, innovation_ref, obs_weight_ref,
-    filtered_ref, adjoint_ref,
-    snd, rcv, ex_src, ex_full, ex_low, ex_high,
+    cell_ref, step_ref, innovation_ref, obs_weight_ref,
+    grad_alpha_ref, grad_control_ref,
+    stage, ens, adjoint, snd, rcv, ex_src, ex_full, ex_low, ex_high,
     send_sem, recv_sem, ex_send, ex_recv,
 ):
     group, part = lax.axis_index("grp"), lax.axis_index("sp")
     left, right = lax.rem(part + parts - 1, parts), lax.rem(part + 1, parts)
-    _, rows, cols = base_ref.shape
-    own, padded = rows // parts, alpha_ref.shape[2]
+    members, rows, cols = alpha_ref.shape
+    own, padded = rows // parts, stage.shape[1]
+    tile_rows = control_ref.shape[1]
+    tile = pl.ds(pl.multiple_of(group * tile_rows, tile_rows), tile_rows)
     items = parts * own * padded
 
     barrier = pltpu.get_barrier_semaphore()
@@ -94,7 +96,26 @@
     for i in range(1, groups):
         for at in (left, part, right):
             pl.semaphore_signal(barrier, inc=1, device_id={"grp": lax.rem(group + i, groups), "sp": at})
+
+    if padded > members:
+        stage[:, members:, :] = jnp.zeros((rows, padded - members, cols), F32)
+        for v in range(3):
+            ens[v, :, members:, :] = jnp.zeros((rows, padded - members, cols), F32)
+    for m in range(members):
+        stage[:, m, :] = alpha_ref[m]
+    snd[0] = stage[...].astype(BF16).reshape(parts, own, padded, cols)
+    cell = cell_ref[...]
+    row = jnp.zeros_like(cell)
+    for r in range(1, rows):
+        row = row + jnp.where(cell >= r * cols * parts, 1, 0)
+    col = cell - row * (cols * parts) - part * cols
+    slot = step_ref[...] * rows + row
+    in_col = (lax.broadcasted_iota(jnp.int32, (cols, cell.shape[1]), 0) == col).astype(F32).astype(BF16)
+    in_slot = lax.broadcasted_iota(jnp.int32, (3 * rows, cell.shape[1]), 0) == slot
     pl.semaphore_wait(barrier, parts - 1 + 3 * (groups - 1))
+    started = []
+    waves = jnp.broadcast_to(weights_ref[...][:, None, :], (parts, own * padded, weights_ref.shape[1]))
+    waves = waves.reshape(items, weights_ref.shape[1])
 
     def all_to_all(phase, source):
         copies = []
@@ -112,8 +133,7 @@
     def finish(copies):
         for copy in copies:
             copy.wait_recv()
-        for copy in copies:
-            copy.wait_send()
+        started.extend(copies)
 
     def filtered(phase):
         x = rcv[phase].reshape(items, cols)
@@ -122,15 +142,13 @@
         re, im = y[:items], y[items:]
         z = right_mul(re * c + im * s, in_hi[:cols], in_lo[:cols])
         z = z + right_mul(im * c - re * s, in_hi[cols:], in_lo[cols:])
-        v = right_mul(z * weights_ref[...], int_hi[...], int_lo[...])
+        v = right_mul(z * waves, int_hi[...], int_lo[...])
         re, im = v[:, :cols], v[:, cols:]
         out = left_mul(bigt_hi[:, :items], bigt_lo[:, :items], re * c - im * s)
         out = out + left_mul(bigt_hi[:, items:], bigt_lo[:, items:], im * c + re * s)
         return out.astype(BF16).reshape(parts, own, padded, cols)
 
-    def exchange(step, fields):
-        for v in range(3):
-            ex_src[step, v] = fields[v]
+    def exchange(step):
         copies = []
         first, last = pl.ds(0, EDGE), pl.ds(cols - EDGE, EDGE)
         for i in range(groups):
@@ -158,15 +176,18 @@
             wide.append(jnp.concatenate(pieces, axis=1))
         return wide
 
-    copies = all_to_all(0, alpha_ref)
-    in_col = (lax.broadcasted_iota(jnp.int32, (cols, col_ref.shape[1]), 0) == col_ref[...]).astype(F32).astype(BF16)
-    in_slot = lax.broadcasted_iota(jnp.int32, (3 * rows, col_ref.shape[1]), 0) == slot_ref[...]
+    copies = all_to_all(0, snd.at[0])
+    for m in range(members):
+        for v in range(3):
+            ens[v, :, m, :] = ensemble_ref[m, v].astype(F32)
     finish(copies)
-    snd[0] = filtered(0)
-    finish(all_to_all(1, snd.at[0]))
+    snd[1] = filtered(0)
+    finish(all_to_all(1, snd.at[1]))
     localized = rcv[1].reshape(rows, padded, cols).astype(F32)
-    partial = [base_ref[v] + spread * jnp.sum(ens_ref[v].astype(F32) * localized, axis=1) for v in range(3)]
-    state0 = exchange(0, partial)
+    for v in range(3):
+        ex_src[0, v] = spread * jnp.sum(ens[v] * localized, axis=1)
+        ex_src[0, v, tile, :] = ex_src[0, v, tile, :] + std_ref[v] * control_ref[v]
+    state0 = exchange(0)
     row_at = lax.broadcasted_iota(jnp.int32, (rows, cols + 2 * EDGE), 0).astype(F32)
     rotation = 0.1 + 0.2 * (row_at + 0.5) / rows
     state1 = model_step(state0, rotation)
@@ -178,21 +199,30 @@
     misfit = obs_weight_ref[...] * (observed - innovation_ref[...])
     high, low = split2(jnp.where(in_slot, misfit, 0.0))
     forcing = dot(high, in_col, ((1,), (1,))) + dot(low, in_col, ((1,), (1,)))
-    forcing = exchange(1, [forcing[t * rows : (t + 1) * rows] for t in range(3)])
+    for t in range(3):
+        ex_src[1, t] = forcing[t * rows : (t + 1) * rows]
+    forcing = exchange(1)
     zero = jnp.zeros_like(rotation)
     h, u, w = adjoint_step((forcing[2], zero, zero), rotation)
     h, u, w = adjoint_step((h + forcing[1], u, w), rotation)
     weighted = jnp.zeros((rows, padded, cols), F32)
     for v, field in enumerate((h + forcing[0], u, w)):
         field = field[:, EDGE:-EDGE]
-        adjoint_ref[v] = field
+        adjoint[v] = field
         half = field.astype(BF16).astype(F32)
-        weighted = weighted + ens_ref[v].astype(F32) * half[:, None, :]
-    snd[1] = weighted.astype(BF16).reshape(parts, own, padded, cols)
-    finish(all_to_all(2, snd.at[1]))
-    snd[2] = filtered(2)
-    finish(all_to_all(3, snd.at[2]))
-    filtered_ref[...] = rcv[3].reshape(rows, padded, cols)
+        weighted = weighted + ens[v] * half[:, None, :]
+    snd[2] = weighted.astype(BF16).reshape(parts, own, padded, cols)
+    copies = all_to_all(2, snd.at[2])
+    for v in range(3):
+        grad_control_ref[v] = control_ref[v] + std_ref[v] * adjoint[v, tile, :]
+    finish(copies)
+    snd[3] = filtered(2)
+    finish(all_to_all(3, snd.at[3]))
+    stage[...] = rcv[3].reshape(rows, padded, cols).astype(F32)
+    for m in range(members):
+        grad_alpha_ref[m] = alpha_ref[m] + spread * stage[:, m, :]
+    for copy in started:
+        copy.wait_send()
 
 
 def both(table):
@@ -204,40 +234,34 @@
     members, rows, cols = alpha.shape
     groups, parts = lax.axis_size("grp"), lax.axis_size("sp")
     spread = 1.0 / math.sqrt(members * groups - 1)
-    tile_rows, own = control.shape[1], rows // parts
+    own = rows // parts
     padded = -(-members // 16) * 16
-    first_row = lax.axis_index("grp") * tile_rows
-    first_col = lax.axis_index("sp") * cols
-    fill = padded - members
 
     outer, tw_c, tw_s, inner = tables(parts, cols, loc_spectrum.shape[0])
     items = own * padded
     big = np.kron(outer, np.eye(items, dtype=np.float32))
     waves = loc_spectrum.reshape(inner.shape[1] // 2, parts).T
-    waves = jnp.repeat(jnp.concatenate([waves, waves], axis=1), items, axis=0)
-    sent = jnp.pad(alpha.astype(BF16).transpose(1, 0, 2), ((0, 0), (0, fill), (0, 0)))
-    ens = jnp.pad(ensemble.transpose(1, 2, 0, 3), ((0, 0), (0, 0), (0, fill), (0, 0)))
-    base = jnp.zeros((3, rows, cols), F32)
-    base = lax.dynamic_update_slice(base, static_std * control, (0, first_row, 0))
-    col = obs_cell % (cols * parts) - first_col
-    slot = obs_step * rows + obs_cell // (cols * parts)
+    waves = jnp.concatenate([waves, waves], axis=1)
     vmem = pl.BlockSpec(memory_space=pltpu.VMEM)
     operands = (
-        sent.reshape(parts, own, padded, cols), ens, base, waves,
+        alpha, ensemble, static_std, control, waves,
         np.repeat(tw_c, items, axis=0), np.repeat(tw_s, items, axis=0),
         *both(big), *both(big.T), *both(inner), *both(inner.T),
-        col[None], slot[None], innovation[None], obs_weight[None],
+        obs_cell[None], obs_step[None], innovation[None], obs_weight[None],
     )
-    filtered, adjoint = pl.pallas_call(
+    return pl.pallas_call(
         functools.partial(kernel, groups, parts, spread),
         out_shape=(
-            jax.ShapeDtypeStruct((rows, padded, cols), BF16),
-            jax.ShapeDtypeStruct((3, rows, cols), F32),
+            jax.ShapeDtypeStruct(alpha.shape, F32),
+            jax.ShapeDtypeStruct(control.shape, F32),
         ),
         in_specs=[vmem] * len(operands),
         out_specs=(vmem, vmem),
         scratch_shapes=[
-            pltpu.VMEM((3, parts, own, padded, cols), BF16),
+            pltpu.VMEM((rows, padded, cols), F32),
+            pltpu.VMEM((3, rows, padded, cols), F32),
+            pltpu.VMEM((3, rows, cols), F32),
+            pltpu.VMEM((4, parts, own, padded, cols), BF16),
             pltpu.VMEM((4, parts, own, padded, cols), BF16),
             pltpu.VMEM((2, 3, rows, cols), F32),
             pltpu.VMEM((2, groups, 3, rows, cols), F32),
@@ -250,10 +274,6 @@
         ],
         compiler_params=pltpu.CompilerParams(collective_id=0, has_side_effects=True, vmem_limit_bytes=60 << 20),
     )(*operands)
-    filtered = filtered[:, :members].transpose(1, 0, 2).astype(F32)
-    grad_alpha = alpha + spread * filtered
-    tile = lax.dynamic_slice_in_dim(adjoint, first_row, tile_rows, axis=1)
-    return grad_alpha, control + static_std * tile
 
 
 def solution(mesh):

time: 52.3 us -> 47 us (0.90)
  local copies, waits for them, and re-layouts: 5.69 us -> 3.03 us
  other arithmetic: 3.07 us -> 0.69 us
    add x3 -> x0, other arithmetic: 2.98 us -> none  [the longest x1 1.36 us: per_device(): return (grad_alpha, control + static_std * tile)]
    pad x1 -> x0, local copies, waits for them, and re-layouts: 0.78 us -> none  [per_device(): jnp.pad(ensemble.transpose(1, 2, 0, 3), ((0, 0), (0, 0), (0, fill), (0, 0)))]
    broadcast_in_dim x2 -> x0, local copies, waits for them, and re-layouts: 0.69 us -> none  [the longest x1 0.68 us: per_device(): waves = jnp.repeat(jnp.concatenate([waves, waves], axis=1), items, axis=0)]
    reshape x1 -> x0, local copies, waits for them, and re-layouts: 0.67 us -> none  [per_device(): sent.reshape(parts, own, padded, cols)]
    concatenate x1, other arithmetic: 0.08 us -> 0.69 us  [per_device(): waves = jnp.concatenate([waves, waves], axis=1)]
    unnamed x16 -> x6, local copies, waits for them, and re-layouts: 3.39 us -> 2.89 us
where the time goes in v3:
time: 47 us; the launch traced here: 46.8 us
  Pallas kernels  42.5 us (90%)
  local copies, waits for them, and re-layouts  3.03 us (6%)
  other arithmetic  0.69 us (1%)
  between operations  0.66 us (1%)
    pallas_call x1, Pallas kernels, per_device(): pl.pallas_call(functools.partial(kernel, groups, parts, spread), out_shap...  42.5 us
    unnamed x6, local copies, waits for them, and re-layouts  2.89 us

profile of v3, /device:TPU:0, one launch (start us, length us, event | category | flops | bytes accessed | tf_op | source)
XLA Modules:
  0.0 46.8 jit_solution(383651817949922511)
XLA Ops:
  0.6 0.0 copy-start.1
  0.6 0.7 %copy-done.1 = f32[1024]{0:T(1024)S(1)} copy-done((f32[1024]{0:T(1024)S(1)}, f32[1024]{0:T(1024)}, u32[]{:S(2)}) %copy-start.1) | copy-done | bytes 4120
  1.3 0.1 reshape.7
  1.4 0.1 copy.21
  1.5 0.7 %pad_maximum_fusion.weights_ref = f32[16,128]{1,0:T(8,128)} fusion(f32[16,64]{1,0:T(8,128)S(1)} %bitcast.5), kind=kLoop, calls=%fused_computation | loop fusion | flops 2048 | bytes 12288 | tf_op jit(solution)/shard_map/concatenate | solution.py:244
  2.1 42.5 %shard_map.194 = (f32[10,16,256]{2,1,0:T(8,128)}, f32[3,8,256]{2,1,0:T(8,128)}) custom-call(f32[10,16,256]{2,1,0:T(8,128)} %alpha_ref.1, bf16[10,3,16,256]{3,2,1,0:T(8,128)(2,1)} %ensemble_ref.1, f32[3,8,256]{2,1,0:T(8,128)} %std_ref.1, f32[3,8,256]{2,1,0:T(8,128)} %control_ref.1, f32[16,128]{1,0:T(8,128)} %pad_maximum_fusion.weights_ref, ...), custom_call_target="tpu_custom_call" | custom-call | tf_op jit(solution)/shard_map/pallas_call | solution.py:252
  44.6 0.0 copy-start
  44.6 1.6 %copy.24 = f32[10,16,256]{2,1,0:T(8,128)} copy(f32[10,16,256]{2,1,0:T(8,128)} %get-tuple-element.4) | data formatting | bytes 327680
  46.2 0.0 copy-done
  46.2 0.6 %copy.25 = f32[3,8,256]{2,1,0:T(8,128)} copy(f32[3,8,256]{2,1,0:T(8,128)S(1)} %copy-done) | data formatting | bytes 49152
Async XLA Ops:
  0.6 0.7 %copy-start.1 = (f32[1024]{0:T(1024)S(1)}, f32[1024]{0:T(1024)}, u32[]{:S(2)}) copy-start(f32[1024]{0:T(1024)} %param.23) | copy-start | bytes 12292
  44.6 1.6 %copy-start = (f32[3,8,256]{2,1,0:T(8,128)S(1)}, f32[3,8,256]{2,1,0:T(8,128)}, u32[]{:S(2)}) copy-start(f32[3,8,256]{2,1,0:T(8,128)} %get-tuple-element.5) | copy-start | bytes 73732

commit v4 on v3

--- a/solution.py
+++ b/solution.py
@@ -75,12 +75,23 @@
 
 def kernel(
     groups, parts, spread,
-    alpha_ref, ensemble_ref, std_ref, control_ref, weights_ref, tw_c_ref, tw_s_ref,
+    alpha_ref, std_ref, control_ref, weights_ref,
+    cell_ref, step_ref, innovation_ref, obs_weight_ref, *refs,
+):
+    far, near = refs[:11], refs[13:24]
+    kernel_body(groups, parts, spread, alpha_ref, std_ref, control_ref, weights_ref, cell_ref, step_ref,
+                innovation_ref, obs_weight_ref, far, near, *near, *refs[11:13], *refs[24:])
+
+
+def kernel_body(
+    groups, parts, spread,
+    alpha_ref, std_ref, control_ref, weights_ref,
+    cell_ref, step_ref, innovation_ref, obs_weight_ref, far, near,
+    ensemble_ref, tw_c_ref, tw_s_ref,
     big_hi, big_lo, bigt_hi, bigt_lo, in_hi, in_lo, int_hi, int_lo,
-    cell_ref, step_ref, innovation_ref, obs_weight_ref,
     grad_alpha_ref, grad_control_ref,
     stage, ens, adjoint, snd, rcv, ex_src, ex_full, ex_low, ex_high,
-    send_sem, recv_sem, ex_send, ex_recv,
+    send_sem, recv_sem, ex_send, ex_recv, load_sem,
 ):
     group, part = lax.axis_index("grp"), lax.axis_index("sp")
     left, right = lax.rem(part + parts - 1, parts), lax.rem(part + 1, parts)
@@ -97,6 +108,9 @@
         for at in (left, part, right):
             pl.semaphore_signal(barrier, inc=1, device_id={"grp": lax.rem(group + i, groups), "sp": at})
 
+    loads = [pltpu.make_async_copy(a, b, load_sem.at[i]) for i, (a, b) in enumerate(zip(far, near))]
+    for load in loads:
+        load.start()
     if padded > members:
         stage[:, members:, :] = jnp.zeros((rows, padded - members, cols), F32)
         for v in range(3):
@@ -177,9 +191,12 @@
         return wide
 
     copies = all_to_all(0, snd.at[0])
+    loads[0].wait()
     for m in range(members):
         for v in range(3):
             ens[v, :, m, :] = ensemble_ref[m, v].astype(F32)
+    for load in loads[1:]:
+        load.wait()
     finish(copies)
     snd[1] = filtered(0)
     finish(all_to_all(1, snd.at[1]))
@@ -244,10 +261,13 @@
     waves = jnp.concatenate([waves, waves], axis=1)
     vmem = pl.BlockSpec(memory_space=pltpu.VMEM)
     operands = (
-        alpha, ensemble, static_std, control, waves,
+        alpha, static_std, control, waves,
+        obs_cell[None], obs_step[None], innovation[None], obs_weight[None],
+    )
+    loaded = (
+        ensemble,
         np.repeat(tw_c, items, axis=0), np.repeat(tw_s, items, axis=0),
         *both(big), *both(big.T), *both(inner), *both(inner.T),
-        obs_cell[None], obs_step[None], innovation[None], obs_weight[None],
     )
     return pl.pallas_call(
         functools.partial(kernel, groups, parts, spread),
@@ -255,9 +275,10 @@
             jax.ShapeDtypeStruct(alpha.shape, F32),
             jax.ShapeDtypeStruct(control.shape, F32),
         ),
-        in_specs=[vmem] * len(operands),
+        in_specs=[vmem] * len(operands) + [pl.BlockSpec(memory_space=pl.ANY)] * len(loaded),
         out_specs=(vmem, vmem),
         scratch_shapes=[
+            *[pltpu.VMEM(t.shape, t.dtype) for t in loaded],
             pltpu.VMEM((rows, padded, cols), F32),
             pltpu.VMEM((3, rows, padded, cols), F32),
             pltpu.VMEM((3, rows, cols), F32),
@@ -271,9 +292,10 @@
             pltpu.SemaphoreType.DMA((4, parts)),
             pltpu.SemaphoreType.DMA((2, 3, groups)),
             pltpu.SemaphoreType.DMA((2, 3, groups)),
+            pltpu.SemaphoreType.DMA((len(loaded),)),
         ],
         compiler_params=pltpu.CompilerParams(collective_id=0, has_side_effects=True, vmem_limit_bytes=60 << 20),
-    )(*operands)
+    )(*operands, *loaded)
 
 
 def solution(mesh):

time: 47 us -> 46.3 us (0.985)
  Pallas kernels: 42.5 us -> 41.8 us
    pallas_call x1, Pallas kernels: 42.5 us -> 41.8 us  [per_device(): pl.pallas_call(functools.partial(kernel, groups, parts, spread), out_shap...]
where the time goes in v4:
time: 46.3 us; the launch traced here: 46.2 us
  Pallas kernels  41.8 us (90%)
  local copies, waits for them, and re-layouts  3.03 us (7%)
  other arithmetic  0.69 us (1%)
  between operations  0.66 us (1%)
    pallas_call x1, Pallas kernels, per_device(): pl.pallas_call(functools.partial(kernel, groups, parts, spread), out_shap...  41.8 us
    unnamed x6, local copies, waits for them, and re-layouts  2.89 us

profile of v4, /device:TPU:0, one launch (start us, length us, event | category | flops | bytes accessed | tf_op | source)
XLA Modules:
  0.0 46.2 jit_solution(12399391641240822939)
XLA Ops:
  0.6 0.0 copy-start.1
  0.6 0.7 %copy-done.1 = f32[1024]{0:T(1024)S(1)} copy-done((f32[1024]{0:T(1024)S(1)}, f32[1024]{0:T(1024)}, u32[]{:S(2)}) %copy-start.1) | copy-done | bytes 4120
  1.3 0.1 reshape.7
  1.4 0.1 copy.21
  1.5 0.7 %pad_maximum_fusion.weights_ref = f32[16,128]{1,0:T(8,128)} fusion(f32[16,64]{1,0:T(8,128)S(1)} %bitcast.5), kind=kLoop, calls=%fused_computation | loop fusion | flops 2048 | bytes 12288 | tf_op jit(solution)/shard_map/concatenate | solution.py:261
  2.1 41.8 %shard_map.194 = (f32[10,16,256]{2,1,0:T(8,128)}, f32[3,8,256]{2,1,0:T(8,128)}) custom-call(f32[10,16,256]{2,1,0:T(8,128)} %alpha_ref.1, f32[3,8,256]{2,1,0:T(8,128)} %std_ref.1, f32[3,8,256]{2,1,0:T(8,128)} %control_ref.1, f32[16,128]{1,0:T(8,128)} %pad_maximum_fusion.weights_ref, s32[1,1024]{1,0:T(1,128)} %bitcast.6, s32[1,1024]{1,0:T(1,128)} %bitcast.7, ...), custom_call_target="tpu_custom_call" | custom-call | tf_op jit(solution)/shard_map/pallas_call | solution.py:272
  43.9 0.0 copy-start
  43.9 1.6 %copy.24 = f32[10,16,256]{2,1,0:T(8,128)} copy(f32[10,16,256]{2,1,0:T(8,128)} %get-tuple-element.4) | data formatting | bytes 327680
  45.5 0.0 copy-done
  45.6 0.6 %copy.25 = f32[3,8,256]{2,1,0:T(8,128)} copy(f32[3,8,256]{2,1,0:T(8,128)S(1)} %copy-done) | data formatting | bytes 49152
Async XLA Ops:
  0.6 0.7 %copy-start.1 = (f32[1024]{0:T(1024)S(1)}, f32[1024]{0:T(1024)}, u32[]{:S(2)}) copy-start(f32[1024]{0:T(1024)} %param.23) | copy-start | bytes 12292
  43.9 1.6 %copy-start = (f32[3,8,256]{2,1,0:T(8,128)S(1)}, f32[3,8,256]{2,1,0:T(8,128)}, u32[]{:S(2)}) copy-start(f32[3,8,256]{2,1,0:T(8,128)} %get-tuple-element.5) | copy-start | bytes 73732
